TPU v7x, 256 devices: a whole 4x4x8 slice. The times are simulated.
256 devices in a mesh: gx: 16 (over y, x), gy: 8 (over z_hi, core), gz: 2 (over z_lo).
Axes of the slice: x: 4, y: 4, z: 8 (z_hi: 4, z_lo: 2; z = z_hi * 2 + z_lo), core: 2. Of those that a mesh axis runs over, the one named last changes fastest.
Arguments:
- head: float32 [16, 1024, 2048], P('gz', 'gx', 'gy'), may hold values from -2 to -0.2
- soil: int32 [16, 1024, 2048], P('gz', 'gx', 'gy'), may hold values from 0 to 7
- boundary: int32 [16, 1024, 2048], P('gz', 'gx', 'gy'), may hold values 0 or 1
- rhs: float32 [16, 1024, 2048], P('gz', 'gx', 'gy'), may hold values from -6 to 6
- soil_alpha: float32 [8], replicated, may hold values from 0.5 to 4
- soil_n: float32 [8], replicated, may hold values from 1.4 to 3
- soil_ks: float32 [8], replicated, may hold values from 0.1 to 2
Outputs:
- update: float32 [16, 1024, 2048], P('gz', 'gx', 'gy')
- residual: float32 [16, 1024, 2048], P('gz', 'gx', 'gy')
Inputs may be any that keep to these rules, and one draw needn't show every extreme that they name: soil indexes the tables soil_alpha, soil_n and soil_ks.
All inputs are finite; a program needn't handle non-finite values. No bound on the sum of `boundary` on one device may be relied on, other than what follows from the above.
Results may differ from a plain program's by a relative error of at most 0.0003.
Values sent between devices are 32-bit elements; how exact they have to be, the bound alone decides.
No kernel may reach another device: no remote copies, remote signals or barrier semaphores. Data moves between devices by JAX's collectives and lax.ppermute only.
A program may use at most 128 MiB of HBM per device.

v0:
```python
import jax
import jax.numpy as jnp
from jax import lax
from jax.experimental import pallas as pl
from jax.experimental.pallas import tpu as pltpu
from jax.sharding import Mesh
from jax.sharding import PartitionSpec as P

AXES = ("gx_0", "gx_1", "gy_0", "gy_1", "gz")
GX = ("gx_0", "gx_1")
GY = ("gy_0", "gy_1")
SOILS = 8
EPS = 1e-06
SPEC = 0.0001
PORE = 0.4
STEP = 0.25
F32 = jnp.float32
NZ, NX, NY = 8, 64, 256
BLOCK = (NZ, NX, NY)
TILES = NX // 8
PARAMS = pltpu.CompilerParams(vmem_limit_bytes=24 * 1024 * 1024)
VMEM = pl.BlockSpec(memory_space=pltpu.VMEM)
SMEM = pl.BlockSpec(memory_space=pltpu.SMEM)


def shape(*dims):
    return jax.ShapeDtypeStruct(dims, F32)


def along(axes):
    index = lax.axis_index(axes[0])
    return index * lax.axis_size(axes[1]) + lax.axis_index(axes[1])


def cell_terms(head, soil, alpha_ref, n_ref, ks_ref):
    alpha = jnp.full(head.shape, alpha_ref[0], F32)
    expo = jnp.full(head.shape, n_ref[0], F32)
    ks = jnp.full(head.shape, ks_ref[0], F32)
    for entry in range(1, SOILS):
        here = soil == entry
        alpha = jnp.where(here, alpha_ref[entry], alpha)
        expo = jnp.where(here, n_ref[entry], expo)
        ks = jnp.where(here, ks_ref[entry], ks)
    depth = -head
    power = 1.0 - 1.0 / expo
    scaled = expo * jnp.log(alpha * depth)
    inverse = jnp.exp(-scaled)
    total = 1.0 + inverse
    part = jnp.log(total)
    root = jnp.exp((-0.5 * power) * (part + scaled))
    bent = jnp.exp(-power * part)
    share = 1.0 / total
    rise = (expo - 1.0) / depth
    gap = 1.0 - bent
    sat = root * root
    conduct = ks * root * gap
    cond = conduct * gap
    dcond = conduct * rise * share * (0.5 * gap + 2.0 * bent * inverse)
    capacity = sat * (SPEC / STEP + (PORE / STEP) * rise * share)
    return cond, dcond, capacity


def couplings(k_own, dk_own, h_own, k_far, dk_far, h_far, tilt):
    part = 1.0 / (k_own + k_far)
    own, far = k_own * part, k_far * part
    slope = h_own - h_far - tilt
    near = 2.0 * far * (k_own + slope * far * dk_own)
    away = -2.0 * own * (k_far - slope * own * dk_far)
    return near, away


def lane_index(dims):
    return lax.broadcasted_iota(jnp.int32, dims, len(dims) - 1)


def row_index(dims):
    return lax.broadcasted_iota(jnp.int32, dims, len(dims) - 2)


def gather_sides(plane, z, odd_x, odd_y, packed):
    low, high = plane[0:1, :], plane[NX - 1 : NX, :]
    row_a = jnp.where(odd_x, low, high)
    row_b = jnp.where(odd_x, high, low)
    col_lane = lane_index((8, 128))
    left, right = plane[:, 0:128], plane[:, 128:256]
    for tile in range(TILES):
        first = jnp.broadcast_to(left[8 * tile : 8 * tile + 8, 0:1], (8, 128))
        last = jnp.broadcast_to(right[8 * tile : 8 * tile + 8, 127:128], (8, 128))
        col_a = jnp.where(odd_y, first, last)
        col_b = jnp.where(odd_y, last, first)
        packed = jnp.where(col_lane == TILES * z + tile, col_a, packed)
        packed = jnp.where(col_lane == TILES * z + tile + 64, col_b, packed)
    return row_a, row_b, packed


def spread_sides(z, odd_x, odd_y, rows_a, rows_b, packed):
    row = row_index((NX, NY))
    at_a = jnp.where(odd_x, 0, NX - 1)
    at_b = jnp.where(odd_x, NX - 1, 0)
    total = jnp.where(row == at_a, rows_a, 0.0) + jnp.where(row == at_b, rows_b, 0.0)
    turned = pltpu.roll(packed, 128 - TILES * z, axis=1)
    pieces = []
    lane = lane_index((8, 128))
    at_first = jnp.where(lane == 0, 1.0, 0.0)
    at_last = jnp.where(lane == 127, 1.0, 0.0)
    for tile in range(TILES):
        col_a = jnp.broadcast_to(turned[:, tile : tile + 1], (8, 128))
        col_b = jnp.broadcast_to(turned[:, tile + 64 : tile + 65], (8, 128))
        first = jnp.where(odd_y, col_a, col_b)
        last = jnp.where(odd_y, col_b, col_a)
        pieces.append(jnp.concatenate([first * at_first, last * at_last], axis=1))
    return total + jnp.concatenate(pieces, axis=0)


def odd_sides():
    return (lax.axis_index("gx_1") % 2) == 1, lax.axis_index("gy_1") == 1


def pack_kernel(head, soil, rhs, z_out, xa_out, xb_out, y_out):
    odd_x, odd_y = odd_sides()
    edge = jnp.where(lax.axis_index("gz") == 0, NZ - 1, 0)
    for slot, ref in enumerate((head, soil, rhs)):
        z_out[slot] = ref[edge].astype(F32)

        def plane_step(z, packed):
            row_a, row_b, packed = gather_sides(ref[z].astype(F32), z, odd_x, odd_y, packed)
            xa_out[slot, pl.ds(z, 1), :] = row_a
            xb_out[slot, pl.ds(z, 1), :] = row_b
            return packed

        y_out[slot] = lax.fori_loop(0, NZ, plane_step, jnp.zeros((8, 128), F32))


def terms_kernel(
    head, soil, rhs, xa, xb, y, alpha, expo, ks, coeffs, image, own_z, own_x, own_y, cond, dcond
):
    edge = jnp.where(lax.axis_index("gz") == 0, NZ - 1, 0)

    def terms_step(z, carry):
        k, dk, capacity = cell_terms(head[z], soil[z], alpha, expo, ks)
        cond[z], dcond[z], coeffs[0, z] = k, dk, capacity
        return carry

    lax.fori_loop(0, NZ, terms_step, 0)
    own_z[0], own_z[1] = cond[edge], dcond[edge]
    for slot, side in enumerate((xa, xb)):
        k, dk, _ = cell_terms(side[0], side[1].astype(jnp.int32), alpha, expo, ks)
        own_x[slot, 0], own_x[slot, 1] = k, dk
    k, dk, _ = cell_terms(y[0], y[1].astype(jnp.int32), alpha, expo, ks)
    own_y[0], own_y[1] = k, dk

    row, lane = row_index((NX, NY)), lane_index((NX, NY))

    def faces_step(z, carry):
        below_near, below_away = carry
        k, dk, h, v = cond[z], dcond[z], head[z], rhs[z]
        above = jnp.minimum(z + 1, NZ - 1)
        under = jnp.maximum(z - 1, 0)
        near, away = couplings(k, dk, h, cond[above], dcond[above], head[above], 1.0)
        inner = jnp.where(z < NZ - 1, 1.0, 0.0)
        near, away = near * inner, away * inner
        diagonal = coeffs[0, z] + near - below_away
        coeffs[1, z] = away
        coeffs[2, z] = -below_near
        total = away * rhs[above] - below_near * rhs[under]
        carry = near, away
        for slot, axis, position in ((3, 0, row), (5, 1, lane)):
            size = k.shape[axis]

            def up(x):
                return pltpu.roll(x, size - 1, axis=axis)

            def down(x):
                return pltpu.roll(x, 1, axis=axis)

            near, away = couplings(k, dk, h, up(k), up(dk), up(h), 0.0)
            inside = position < size - 1
            near, away = jnp.where(inside, near, 0.0), jnp.where(inside, away, 0.0)
            past = -down(near)
            diagonal = diagonal + near - down(away)
            coeffs[slot, z] = away
            coeffs[slot + 1, z] = past
            total = total + away * up(v) + past * down(v)
        coeffs[0, z] = diagonal
        image[z] = total + diagonal * v
        return carry

    nothing = jnp.zeros((NX, NY), F32)
    lax.fori_loop(0, NZ, faces_step, (nothing, nothing))


def pick_y(y_a, y_b):
    return jnp.where(lane_index(y_a.shape) < 64, y_a, y_b)


def first_kernel(
    head, boundary, rhs, interior, z_own, xa_own, xb_own, y_own, own_z, own_x, own_y,
    z_far, xa_far, xb_far, ya_far, yb_far, alpha, expo, ks,
    image, z_out, xa_out, xb_out, y_out, face_z, face_x, face_y,
):
    odd_x, odd_y = odd_sides()
    gz = lax.axis_index("gz")
    edge = jnp.where(gz == 0, NZ - 1, 0)
    tilt = jnp.where(gz == 0, 1.0, -1.0)
    gx, gy = along(GX), along(GY)
    has_x = jnp.logical_and(gx > 0, gx < lax.axis_size(GX) - 1)
    has_y = jnp.logical_and(gy > 0, gy < lax.axis_size(GY) - 1)

    def face(own, own_terms, far, there, slant):
        far_head = far[0] if there is None else jnp.where(there, far[0], -1.0)
        k, dk, _ = cell_terms(far_head, far[1].astype(jnp.int32), alpha, expo, ks)
        near, away = couplings(own_terms[0], own_terms[1], own[0], k, dk, far_head, slant)
        if there is not None:
            near, away = jnp.where(there, near, 0.0), jnp.where(there, away, 0.0)
        return near, away, near * own[2] + away * far[2]

    lane = lane_index((8, 128))
    far_y = tuple(pick_y(ya_far[slot], yb_far[slot]) for slot in range(3))
    there_y = jnp.logical_or(lane < 64, has_y)
    near, away, sum_y = face((y_own[0], None, y_own[2]), (own_y[0], own_y[1]), far_y, there_y, 0.0)
    face_y[0], face_y[1] = near, away
    sums_x = []
    for slot, (own, far, there) in enumerate(((xa_own, xa_far, None), (xb_own, xb_far, has_x))):
        near, away, total = face(own, (own_x[slot, 0], own_x[slot, 1]), far, there, 0.0)
        face_x[slot, 0], face_x[slot, 1] = near, away
        sums_x.append(total)
    near, away, sum_z = face(z_own, (own_z[0], own_z[1]), z_far, None, tilt)
    face_z[0], face_z[1] = near, away
    xa_out[...], xb_out[...] = sums_x
    image[...] = interior[...]
    image[edge] = image[edge] + sum_z

    def plane_step(z, packed):
        total = image[z] + spread_sides(
            z, odd_x, odd_y, xa_out[pl.ds(z, 1), :], xb_out[pl.ds(z, 1), :], sum_y
        )
        plane = jnp.where(boundary[z] == 1, rhs[z], total)
        image[z] = plane
        row_a, row_b, packed = gather_sides(plane, z, odd_x, odd_y, packed)
        xa_out[pl.ds(z, 1), :] = row_a
        xb_out[pl.ds(z, 1), :] = row_b
        return packed

    y_out[...] = lax.fori_loop(0, NZ, plane_step, jnp.zeros((8, 128), F32))
    z_out[...] = image[edge]


def fold(x):
    total = x[0:8, 0:128] + x[0:8, 128:256]
    for tile in range(1, TILES):
        total = total + x[8 * tile : 8 * tile + 8, 0:128] + x[8 * tile : 8 * tile + 8, 128:256]
    return total


def inner_kernel(coeffs, v_ref, rhs, interior, partial):
    def plane_step(z, sums):
        v, start = v_ref[z], rhs[z]
        above = jnp.minimum(z + 1, NZ - 1)
        under = jnp.maximum(z - 1, 0)
        total = coeffs[0, z] * v + coeffs[1, z] * v_ref[above] + coeffs[2, z] * v_ref[under]
        total = total + coeffs[3, z] * pltpu.roll(v, NX - 1, axis=0)
        total = total + coeffs[4, z] * pltpu.roll(v, 1, axis=0)
        total = total + coeffs[5, z] * pltpu.roll(v, NY - 1, axis=1)
        total = total + coeffs[6, z] * pltpu.roll(v, 1, axis=1)
        interior[z] = total
        products = (start * start, start * v, v * v)
        return tuple(s + fold(p) for s, p in zip(sums, products, strict=True))

    sums = lax.fori_loop(0, NZ, plane_step, (jnp.zeros((8, 128), F32),) * 3)
    for slot in range(3):
        partial[slot] = sums[slot]


def second_kernel(
    boundary, rhs, v_ref, interior, partial, z_own, xa_own, xb_own, y_own,
    z_far, xa_far, xb_far, ya_far, yb_far, face_z, face_x, face_y,
    image, sums_out, xa_sum, xb_sum,
):
    odd_x, odd_y = odd_sides()
    edge = jnp.where(lax.axis_index("gz") == 0, NZ - 1, 0)
    sum_y = face_y[0] * y_own[...] + face_y[1] * pick_y(ya_far[...], yb_far[...])
    xa_sum[...] = face_x[0, 0] * xa_own[...] + face_x[0, 1] * xa_far[...]
    xb_sum[...] = face_x[1, 0] * xb_own[...] + face_x[1, 1] * xb_far[...]
    image[...] = interior[...]
    image[edge] = image[edge] + face_z[0] * z_own[...] + face_z[1] * z_far[...]

    def plane_step(z, sums):
        v = v_ref[z]
        total = image[z] + spread_sides(
            z, odd_x, odd_y, xa_sum[pl.ds(z, 1), :], xb_sum[pl.ds(z, 1), :], sum_y
        )
        plane = jnp.where(boundary[z] == 1, v, total)
        image[z] = plane
        products = (plane * rhs[z], plane * v, plane * plane)
        return tuple(s + fold(p) for s, p in zip(sums, products, strict=True))

    sums = lax.fori_loop(0, NZ, plane_step, (jnp.zeros((8, 128), F32),) * 3)
    lane = lane_index((1, 8))
    row = jnp.zeros((1, 8), F32)
    for slot, part in enumerate((partial[0], partial[1], partial[2]) + sums):
        value = jnp.sum(jnp.sum(part, axis=0, keepdims=True), axis=1, keepdims=True)
        row = jnp.where(lane == slot, value, row)
    sums_out[...] = jnp.broadcast_to(row, sums_out.shape)


def least_squares(hess, beta):
    count = len(hess)
    rows = count + 1
    nothing = jnp.zeros_like(beta)
    columns = [[h[i] if i < len(h) else nothing for i in range(rows)] for h in hess]
    basis_q = []
    upper_r = [[None] * count for _ in range(count)]
    for column in range(count):
        vector = columns[column]
        for row in range(column):
            products = [q * c for q, c in zip(basis_q[row], columns[column], strict=True)]
            upper_r[row][column] = sum(products[1:], products[0])
        for row in range(column):
            scale = upper_r[row][column]
            vector = [v - scale * q for v, q in zip(vector, basis_q[row], strict=True)]
        squares = [v * v for v in vector]
        upper_r[column][column] = jnp.sqrt(sum(squares[1:], squares[0]))
        basis_q.append([v / upper_r[column][column] for v in vector])
    target = [beta * basis_q[row][0] for row in range(count)]
    solved = [None] * count
    for row in range(count - 1, -1, -1):
        value = target[row]
        for column in range(row + 1, count):
            value = value - upper_r[row][column] * solved[column]
        solved[row] = value / upper_r[row][row]
    return solved


def combine_kernel(rhs, first, second, sums, update, residual):
    total = jnp.sum(sums[...], axis=0, keepdims=True)
    g00, g01, g11, g02, g12, g22 = (total[:, i : i + 1] for i in range(6))
    square = g00 + EPS
    beta = jnp.sqrt(square)
    h00 = g01 / square
    rest = (g11 - 2.0 * h00 * g01 + h00 * h00 * g00) / square
    rest = jnp.maximum(rest, 0.0)
    h10 = jnp.sqrt(rest + EPS)
    h01 = (g02 - h00 * g01) / (square * h10)
    scale = square * h10 * h10
    h11 = (g12 - h00 * (g02 + g11 - h00 * g01)) / scale
    norm_w = (g22 - 2.0 * h00 * g12 + h00 * h00 * g11) / scale
    v00 = g00 / square
    v01 = (g01 - h00 * g00) / (square * h10)
    v11 = rest / (h10 * h10)
    last = norm_w - 2.0 * (h01 * h01 + h11 * h11)
    last = last + h01 * h01 * v00 + 2.0 * h01 * h11 * v01 + h11 * h11 * v11
    h21 = jnp.sqrt(jnp.maximum(last, 0.0) + EPS)
    y0, y1 = least_squares([[h00, h10], [h01, h11, h21]], beta)
    step = y1 / (beta * h10)
    base = y0 / beta - h00 * step

    def plane_step(z, carry):
        a, b, c = rhs[z], first[z], second[z]
        update[z] = base * a + step * b
        residual[z] = a - (base * b + step * c)
        return carry

    lax.fori_loop(0, NZ, plane_step, 0)


def cost(flops):
    return pl.CostEstimate(flops=flops, bytes_accessed=4 * 1024 * 1024, transcendentals=0)


def swap(x, axis, start, count):
    pairs = [(i, i + 1) for i in range(start, count - 1, 2)]
    return lax.ppermute(x, axis, pairs + [(b, a) for a, b in pairs])


def exchange(z, xa, xb, y):
    count_x, count_y = lax.axis_size(GX), lax.axis_size(GY)
    return (
        swap(z, "gz", 0, 2),
        swap(xa, GX, 0, count_x),
        swap(xb, GX, 1, count_x),
        swap(y, GY, 0, count_y),
        swap(y, GY, 1, count_y),
    )


def call(kernel, ins, outs, flops, scratch=()):
    return pl.pallas_call(
        kernel,
        out_shape=outs,
        in_specs=ins,
        out_specs=jax.tree.map(lambda _: VMEM, outs),
        scratch_shapes=list(scratch),
        compiler_params=PARAMS,
        cost_estimate=cost(flops),
        name=kernel.__name__,
    )


def body(head, soil, boundary, rhs, soil_alpha, soil_n, soil_ks):
    tables = (soil_alpha, soil_n, soil_ks)
    sides = (shape(3, NX, NY), shape(3, 8, NY), shape(3, 8, NY), shape(3, 8, 128))
    z, xa, xb, y = call(pack_kernel, [VMEM] * 3, sides, 1000000)(head, soil, rhs)
    far = exchange(z, xa, xb, y)
    own = (shape(2, NX, NY), shape(2, 2, 8, NY), shape(2, 8, 128))
    coeffs, interior, own_z, own_x, own_y = call(
        terms_kernel,
        [VMEM] * 6 + [SMEM] * 3,
        (shape(7, *BLOCK), shape(*BLOCK)) + own,
        40000000,
        (pltpu.VMEM(BLOCK, F32), pltpu.VMEM(BLOCK, F32)),
    )(head, soil, rhs, xa, xb, y, *tables)
    sides = (shape(NX, NY), shape(8, NY), shape(8, NY), shape(8, 128))
    first, z1, xa1, xb1, y1, face_z, face_x, face_y = call(
        first_kernel,
        [VMEM] * 16 + [SMEM] * 3,
        (shape(*BLOCK),) + sides + own,
        8000000,
    )(head, boundary, rhs, interior, z, xa, xb, y, own_z, own_x, own_y, *far, *tables)
    far = exchange(z1, xa1, xb1, y1)
    interior, partial = call(
        inner_kernel, [VMEM] * 3, (shape(*BLOCK), shape(3, 8, 128)), 8000000
    )(coeffs, first, rhs)
    second, sums = call(
        second_kernel,
        [VMEM] * 17,
        (shape(*BLOCK), shape(256, 8)),
        8000000,
        (pltpu.VMEM((8, NY), F32), pltpu.VMEM((8, NY), F32)),
    )(boundary, rhs, first, interior, partial, z1, xa1, xb1, y1, *far, face_z, face_x, face_y)
    sums = lax.all_to_all(sums, AXES, 0, 0)
    return call(combine_kernel, [VMEM] * 4, (shape(*BLOCK), shape(*BLOCK)), 1000000)(
        rhs, first, second, sums
    )


def solution(mesh):
    split = Mesh(mesh.devices.reshape(4, 4, 4, 2, mesh.shape["gz"]), AXES)
    in_specs = (P("gz", GX, GY),) * 4 + (P(), P(), P())
    out_specs = (P("gz", GX, GY), P("gz", GX, GY))
    return jax.shard_map(body, mesh=split, in_specs=in_specs, out_specs=out_specs, check_vma=False)
```

profile of v0, /device:TPU:1, one launch (start us, length us, event | category | flops | bytes accessed | tf_op | source)
XLA Modules:
  0.0 70.8 jit_solution(9734331015957324192)
XLA Ops:
  0.6 0.0 copy-start
  0.6 1.0 %copy-done = f32[8,64,256]{2,1,0:T(8,128)S(1)} copy-done((f32[8,64,256]{2,1,0:T(8,128)S(1)}, f32[8,64,256]{2,1,0:T(8,128)}, u32[]{:S(2)}) %copy-start) | copy-done | bytes 524312
  1.7 0.0 copy-start.3
  1.7 1.0 %copy-done.3 = f32[8,64,256]{2,1,0:T(8,128)S(1)} copy-done((f32[8,64,256]{2,1,0:T(8,128)S(1)}, f32[8,64,256]{2,1,0:T(8,128)}, u32[]{:S(2)}) %copy-start.3) | copy-done | bytes 524312
  2.7 0.0 copy-start.4
  2.7 1.0 %copy-done.4 = s32[8,64,256]{2,1,0:T(8,128)S(1)} copy-done((s32[8,64,256]{2,1,0:T(8,128)S(1)}, s32[8,64,256]{2,1,0:T(8,128)}, u32[]{:S(2)}) %copy-start.4) | copy-done | bytes 524312
  3.8 0.0 copy-start.2
  3.8 2.1 %pack_kernel.1 = (f32[3,64,256]{2,1,0:T(8,128)S(1)}, f32[3,8,256]{2,1,0:T(8,128)S(1)}, f32[3,8,256]{2,1,0:T(8,128)S(1)}, f32[3,8,128]{2,1,0:T(8,128)S(1)}) custom-call(f32[8,64,256]{2,1,0:T(8,128)S(1)} %copy-done.3, s32[8,64,256]{2,1,0:T(8,128)S(1)} %copy-done.4, f32[8,64,256]{2,1,0:T(8,128)S(1)} %copy-done), custom_call_target="tpu_custom_call" | custom-call | flops 1000000 | bytes 4194304 | tf_op jit(solution)/shard_map/pack_kernel/pallas_call | solution.py:402
  5.9 2.5 %collective-permute-start = (f32[3,64,256]{2,1,0:T(8,128)S(1)}, f32[3,64,256]{2,1,0:T(8,128)S(1)}, u32[]{:S(2)}, u32[]{:S(2)}) collective-permute-start(f32[3,64,256]{2,1,0:T(8,128)S(1)} %get-tuple-element.27.z_own), channel_id=1, source_target_pairs={{0,1},{1,0},{2,3},{3,2},{4,5},{5,4},{6,7},{7,6},{8,9},{9,8},{10,11... | collective-permute-start | bytes 589832 | tf_op jit(solution)/shard_map/ppermute | solution.py:372
  8.4 1.2 %collective-permute-start.1 = (f32[3,8,256]{2,1,0:T(8,128)S(1)}, f32[3,8,256]{2,1,0:T(8,128)S(1)}, u32[]{:S(2)}, u32[]{:S(2)}) collective-permute-start(f32[3,8,256]{2,1,0:T(8,128)S(1)} %get-tuple-element.23.xa.xa_own), channel_id=1, source_target_pairs={{0,16},{32,48},{64,80},{96,112},{128,144},{160,176},{192,208},{224... | collective-permute-start | bytes 73736 | tf_op jit(solution)/shard_map/ppermute | solution.py:372
  9.6 0.7 collective-permute-start.2
  10.3 6.0 %collective-permute-start.4 = (f32[3,8,128]{2,1,0:T(8,128)S(1)}, f32[3,8,128]{2,1,0:T(8,128)S(1)}, u32[]{:S(2)}, u32[]{:S(2)}) collective-permute-start(f32[3,8,128]{2,1,0:T(8,128)S(1)} %get-tuple-element.25.y.y_own), channel_id=1, source_target_pairs={{2,4},{6,8},{10,12},{4,2},{8,6},{12,10},{3,5},{7,9},{11,13},{5,3},... | collective-permute-start | bytes 36872 | tf_op jit(solution)/shard_map/ppermute | solution.py:372
  16.3 0.1 collective-permute-start.3
  16.4 0.0 copy-start.7
  16.4 0.6 copy-done.7
  17.1 0.0 copy-start.8
  17.1 0.7 copy-done.8
  17.7 0.0 copy-start.9
  17.7 0.7 copy-done.9
  18.4 4.1 %terms_kernel.1 = (f32[7,8,64,256]{3,2,1,0:T(8,128)S(1)}, f32[8,64,256]{2,1,0:T(8,128)S(1)}, f32[2,64,256]{2,1,0:T(8,128)S(1)}, f32[2,2,8,256]{3,2,1,0:T(8,128)S(1)}, f32[2,8,128]{2,1,0:T(8,128)S(1)}) custom-call(f32[8,64,256]{2,1,0:T(8,128)S(1)} %copy-done.3, s32[8,64,256]{2,1,0:T(8,128)S(1)} %copy-done.4, f32[8,64,256]{2,1,0:T(8,128)S(1)} %copy-done, ...), custom_call_target="tpu_custom_call" | custom-call | flops 40000000 | bytes 4194304 | tf_op jit(solution)/shard_map/terms_kernel/pallas_call | solution.py:405
  22.5 0.0 collective-permute-done.4.yb_far
  22.5 0.0 collective-permute-done.3.ya_far
  22.5 0.0 collective-permute-done.1.xa_far
  22.5 0.0 collective-permute-done.2.xb_far
  22.5 0.0 collective-permute-done.z_far
  22.5 0.0 copy-start.1
  22.6 1.0 %copy-done.1 = f32[8,64,256]{2,1,0:T(8,128)S(1)} copy-done((f32[8,64,256]{2,1,0:T(8,128)S(1)}, f32[8,64,256]{2,1,0:T(8,128)}, u32[]{:S(2)}) %copy-start.1) | copy-done | bytes 524312
  23.6 0.0 copy-start.5
  23.6 1.0 %copy-done.5 = s32[8,64,256]{2,1,0:T(8,128)S(1)} copy-done((s32[8,64,256]{2,1,0:T(8,128)S(1)}, s32[8,64,256]{2,1,0:T(8,128)}, u32[]{:S(2)}) %copy-start.5) | copy-done | bytes 524312
  24.6 0.0 copy-start.6
  24.6 2.8 %first_kernel.1 = (f32[8,64,256]{2,1,0:T(8,128)S(1)}, f32[64,256]{1,0:T(8,128)S(1)}, f32[8,256]{1,0:T(8,128)S(1)}, f32[8,256]{1,0:T(8,128)S(1)}, f32[8,128]{1,0:...) custom-call(f32[8,64,256]{2,1,0:T(8,128)S(1)} %copy-done.3, ...), custom_call_target="tpu_custom_call" | custom-call | flops 8000000 | bytes 4194304 | tf_op jit(solution)/shard_map/first_kernel/pallas_call | solution.py:413
  27.4 0.1 collective-permute-start.5
  27.5 3.7 %collective-permute-start.6 = (f32[8,256]{1,0:T(8,128)S(1)}, f32[8,256]{1,0:T(8,128)S(1)}, u32[]{:S(2)}, u32[]{:S(2)}) collective-permute-start(f32[8,256]{1,0:T(8,128)S(1)} %get-tuple-element.36.xa_own), channel_id=1, source_target_pairs={{0,16},{32,48},{64,80},{96,112},{128,144},{160,176},{192,208},{224... | collective-permute-start | bytes 24584 | tf_op jit(solution)/shard_map/ppermute | solution.py:372
  31.3 0.6 collective-permute-start.7
  31.9 6.8 %collective-permute-start.9 = (f32[8,128]{1,0:T(8,128)S(1)}, f32[8,128]{1,0:T(8,128)S(1)}, u32[]{:S(2)}, u32[]{:S(2)}) collective-permute-start(f32[8,128]{1,0:T(8,128)S(1)} %get-tuple-element.38.y_own), channel_id=1, source_target_pairs={{2,4},{6,8},{10,12},{4,2},{8,6},{12,10},{3,5},{7,9},{11,13},{5,3},... | collective-permute-start | bytes 12296 | tf_op jit(solution)/shard_map/ppermute | solution.py:372
  38.7 0.1 collective-permute-start.8
  38.8 0.0 copy-done.2
  38.8 0.8 %inner_kernel.1 = (f32[8,64,256]{2,1,0:T(8,128)S(1)}, f32[3,8,128]{2,1,0:T(8,128)S(1)}) custom-call(f32[7,8,64,256]{3,2,1,0:T(8,128)S(1)} %get-tuple-element.32.coeffs, f32[8,64,256]{2,1,0:T(8,128)S(1)} %get-tuple-element.31.v_ref.first, f32[8,64,256]{2,1,0:T(8,128)S(1)} %copy-done.2), custom_call_target="tpu_custom_call" | custom-call | flops 8000000 | bytes 4194304 | tf_op jit(solution)/shard_map/inner_kernel/pallas_call | solution.py:420
  39.7 0.3 collective-permute-done.9.yb_far
  40.0 0.0 collective-permute-done.8.ya_far
  40.0 0.0 collective-permute-done.6.xa_far
  40.0 0.0 collective-permute-done.7.xb_far
  40.0 0.0 collective-permute-done.5.z_far
  40.0 0.0 copy-done.6
  40.0 1.5 %second_kernel.1 = (f32[8,64,256]{2,1,0:T(8,128)S(1)}, f32[256,8]{1,0:T(8,128)S(1)}) custom-call(s32[8,64,256]{2,1,0:T(8,128)S(1)} %copy-done.6, f32[8,64,256]{2,1,0:T(8,128)S(1)} %copy-done.2, f32[8,64,256]{2,1,0:T(8,128)S(1)} %get-tuple-element.31.v_ref.first, f32[8,64,256]{2,1,0:T(8,128)S(1)} %get-tuple-element.33.interior, ...), custom_call_target="tpu_custom_call" | custom-call | flops 8000000 | bytes 4194304 | tf_op jit(solution)/shard_map/second_kernel/pallas_call | solution.py:423
  41.6 26.9 %all_to_all.11 = f32[256,1,8]{2,1,0:T(1,128)S(1)} all-to-all(f32[256,1,8]{2,1,0:T(1,128)S(1)} %bitcast.5), channel_id=1, replica_groups=mesh['gx_0'=4,'gx_1'=4,'gy_0'=4,'gy_1'=2,'gz'=2] {'gx_0','gx_1','gy_0','..., dimensions={0} | all-to-all | bytes 16384 | tf_op jit(solution)/shard_map/all_to_all | solution.py:430
  68.4 2.4 %combine_kernel.1 = (f32[8,64,256]{2,1,0:T(8,128)}, f32[8,64,256]{2,1,0:T(8,128)}) custom-call(f32[8,64,256]{2,1,0:T(8,128)S(1)} %copy-done.2, f32[8,64,256]{2,1,0:T(8,128)S(1)} %get-tuple-element.31.v_ref.first, f32[8,64,256]{2,1,0:T(8,128)S(1)} %get-tuple-element.42.second, f32[256,8]{1,0:T(8,128)S(1)} %bitcast.4), custom_call_target="tpu_custom_call" | custom-call | flops 1000000 | bytes 4194304 | tf_op jit(solution)/shard_map/combine_kernel/pallas_call | solution.py:431
Async XLA Ops:
  0.6 1.0 %copy-start = (f32[8,64,256]{2,1,0:T(8,128)S(1)}, f32[8,64,256]{2,1,0:T(8,128)}, u32[]{:S(2)}) copy-start(f32[8,64,256]{2,1,0:T(8,128)} %rhs.11) | copy-start | bytes 1572868
  1.7 1.0 %copy-start.3 = (f32[8,64,256]{2,1,0:T(8,128)S(1)}, f32[8,64,256]{2,1,0:T(8,128)}, u32[]{:S(2)}) copy-start(f32[8,64,256]{2,1,0:T(8,128)} %head.5) | copy-start | bytes 1572868
  2.7 1.0 %copy-start.4 = (s32[8,64,256]{2,1,0:T(8,128)S(1)}, s32[8,64,256]{2,1,0:T(8,128)}, u32[]{:S(2)}) copy-start(s32[8,64,256]{2,1,0:T(8,128)} %soil.3) | copy-start | bytes 1572868
  3.8 35.0 %copy-start.2 = (f32[8,64,256]{2,1,0:T(8,128)S(1)}, f32[8,64,256]{2,1,0:T(8,128)}, u32[]{:S(2)}) copy-start(f32[8,64,256]{2,1,0:T(8,128)} %rhs.11) | copy-start | bytes 1572868
  5.9 16.7 %collective-permute-start = (f32[3,64,256]{2,1,0:T(8,128)S(1)}, f32[3,64,256]{2,1,0:T(8,128)S(1)}, u32[]{:S(2)}, u32[]{:S(2)}) collective-permute-start(f32[3,64,256]{2,1,0:T(8,128)S(1)} %get-tuple-element.27.z_own), channel_id=1, source_target_pairs={{0,1},{1,0},{2,3},{3,2},{4,5},{5,4},{6,7},{7,6},{8,9},{9,8},{10,11... | collective-permute-start | bytes 589832 | tf_op jit(solution)/shard_map/ppermute | solution.py:372
  8.4 14.1 %collective-permute-start.1 = (f32[3,8,256]{2,1,0:T(8,128)S(1)}, f32[3,8,256]{2,1,0:T(8,128)S(1)}, u32[]{:S(2)}, u32[]{:S(2)}) collective-permute-start(f32[3,8,256]{2,1,0:T(8,128)S(1)} %get-tuple-element.23.xa.xa_own), channel_id=1, source_target_pairs={{0,16},{32,48},{64,80},{96,112},{128,144},{160,176},{192,208},{224... | collective-permute-start | bytes 73736 | tf_op jit(solution)/shard_map/ppermute | solution.py:372
  9.6 12.9 %collective-permute-start.2 = (f32[3,8,256]{2,1,0:T(8,128)S(1)}, f32[3,8,256]{2,1,0:T(8,128)S(1)}, u32[]{:S(2)}, u32[]{:S(2)}) collective-permute-start(f32[3,8,256]{2,1,0:T(8,128)S(1)} %get-tuple-element.24.xb.xb_own), channel_id=1, source_target_pairs={{16,32},{48,64},{80,96},{112,128},{144,160},{176,192},{208,224},{3... | collective-permute-start | bytes 73736 | tf_op jit(solution)/shard_map/ppermute | solution.py:372
  10.3 12.2 %collective-permute-start.4 = (f32[3,8,128]{2,1,0:T(8,128)S(1)}, f32[3,8,128]{2,1,0:T(8,128)S(1)}, u32[]{:S(2)}, u32[]{:S(2)}) collective-permute-start(f32[3,8,128]{2,1,0:T(8,128)S(1)} %get-tuple-element.25.y.y_own), channel_id=1, source_target_pairs={{2,4},{6,8},{10,12},{4,2},{8,6},{12,10},{3,5},{7,9},{11,13},{5,3},... | collective-permute-start | bytes 36872 | tf_op jit(solution)/shard_map/ppermute | solution.py:372
  16.3 6.2 %collective-permute-start.3 = (f32[3,8,128]{2,1,0:T(8,128)S(1)}, f32[3,8,128]{2,1,0:T(8,128)S(1)}, u32[]{:S(2)}, u32[]{:S(2)}) collective-permute-start(f32[3,8,128]{2,1,0:T(8,128)S(1)} %get-tuple-element.25.y.y_own), channel_id=1, source_target_pairs={{0,2},{4,6},{8,10},{12,14},{2,0},{6,4},{10,8},{14,12},{1,3},{5,7},... | collective-permute-start | bytes 36872 | tf_op jit(solution)/shard_map/ppermute | solution.py:372
  16.4 0.7 copy-start.7
  17.1 0.7 copy-start.8
  17.7 0.7 copy-start.9
  22.5 1.0 %copy-start.1 = (f32[8,64,256]{2,1,0:T(8,128)S(1)}, f32[8,64,256]{2,1,0:T(8,128)}, u32[]{:S(2)}) copy-start(f32[8,64,256]{2,1,0:T(8,128)} %rhs.11) | copy-start | bytes 1572868
  23.6 1.0 %copy-start.5 = (s32[8,64,256]{2,1,0:T(8,128)S(1)}, s32[8,64,256]{2,1,0:T(8,128)}, u32[]{:S(2)}) copy-start(s32[8,64,256]{2,1,0:T(8,128)} %boundary.3) | copy-start | bytes 1572868
  24.6 15.4 %copy-start.6 = (s32[8,64,256]{2,1,0:T(8,128)S(1)}, s32[8,64,256]{2,1,0:T(8,128)}, u32[]{:S(2)}) copy-start(s32[8,64,256]{2,1,0:T(8,128)} %boundary.3) | copy-start | bytes 1572868
  27.4 12.6 %collective-permute-start.5 = (f32[64,256]{1,0:T(8,128)S(1)}, f32[64,256]{1,0:T(8,128)S(1)}, u32[]{:S(2)}, u32[]{:S(2)}) collective-permute-start(f32[64,256]{1,0:T(8,128)S(1)} %get-tuple-element.35.z_own), channel_id=1, source_target_pairs={{0,1},{1,0},{2,3},{3,2},{4,5},{5,4},{6,7},{7,6},{8,9},{9,8},{10,11... | collective-permute-start | bytes 196616 | tf_op jit(solution)/shard_map/ppermute | solution.py:372
  27.5 12.5 %collective-permute-start.6 = (f32[8,256]{1,0:T(8,128)S(1)}, f32[8,256]{1,0:T(8,128)S(1)}, u32[]{:S(2)}, u32[]{:S(2)}) collective-permute-start(f32[8,256]{1,0:T(8,128)S(1)} %get-tuple-element.36.xa_own), channel_id=1, source_target_pairs={{0,16},{32,48},{64,80},{96,112},{128,144},{160,176},{192,208},{224... | collective-permute-start | bytes 24584 | tf_op jit(solution)/shard_map/ppermute | solution.py:372
  31.3 8.7 %collective-permute-start.7 = (f32[8,256]{1,0:T(8,128)S(1)}, f32[8,256]{1,0:T(8,128)S(1)}, u32[]{:S(2)}, u32[]{:S(2)}) collective-permute-start(f32[8,256]{1,0:T(8,128)S(1)} %get-tuple-element.37.xb_own), channel_id=1, source_target_pairs={{16,32},{48,64},{80,96},{112,128},{144,160},{176,192},{208,224},{3... | collective-permute-start | bytes 24584 | tf_op jit(solution)/shard_map/ppermute | solution.py:372
  31.9 8.1 %collective-permute-start.9 = (f32[8,128]{1,0:T(8,128)S(1)}, f32[8,128]{1,0:T(8,128)S(1)}, u32[]{:S(2)}, u32[]{:S(2)}) collective-permute-start(f32[8,128]{1,0:T(8,128)S(1)} %get-tuple-element.38.y_own), channel_id=1, source_target_pairs={{2,4},{6,8},{10,12},{4,2},{8,6},{12,10},{3,5},{7,9},{11,13},{5,3},... | collective-permute-start | bytes 12296 | tf_op jit(solution)/shard_map/ppermute | solution.py:372
  38.7 1.3 %collective-permute-start.8 = (f32[8,128]{1,0:T(8,128)S(1)}, f32[8,128]{1,0:T(8,128)S(1)}, u32[]{:S(2)}, u32[]{:S(2)}) collective-permute-start(f32[8,128]{1,0:T(8,128)S(1)} %get-tuple-element.38.y_own), channel_id=1, source_target_pairs={{0,2},{4,6},{8,10},{12,14},{2,0},{6,4},{10,8},{14,12},{1,3},{5,7},... | collective-permute-start | bytes 12296 | tf_op jit(solution)/shard_map/ppermute | solution.py:372
where the time goes:
time: 71.2 us; the launch traced here: 70.8 us
  blocking collectives  26.9 us (38%)
  starting transfers between devices  21.9 us (31%)
  Pallas kernels  13.7 us (19%)
  local copies, waits for them, and re-layouts  7.16 us (10%)
  between operations  0.82 us (1%)
    all_to_all x1, blocking collectives, body(): sums = lax.all_to_all(sums, AXES, 0, 0)  26.9 us
    ppermute x10, starting transfers between devices, swap(): return lax.ppermute(x, axis, pairs + [(b, a) for a, b in pairs])  21.9 us
    unnamed x20, local copies, waits for them, and re-layouts  7.16 us
    pallas_call x1, Pallas kernels, body(): call(terms_kernel, [VMEM] * 6 + [SMEM] * 3, (shape(7, *BLOCK), shape(*BLO...  4.11 us
    pallas_call x1, Pallas kernels, body(): call(first_kernel, [VMEM] * 16 + [SMEM] * 3, (shape(*BLOCK),) + sides + o...  2.77 us
    pallas_call x1, Pallas kernels, body(): call(combine_kernel, [VMEM] * 4, (shape(*BLOCK), shape(*BLOCK)), 1000000)  2.35 us
    pallas_call x1, Pallas kernels, body(): call(pack_kernel, [VMEM] * 3, sides, 1000000)(head, soil, rhs)  2.1 us
    pallas_call x1, Pallas kernels, body(): call(second_kernel, [VMEM] * 17, (shape(*BLOCK), shape(256, 8)), 8000000,...  1.54 us
  transfers between devices with their start and end apart: 10, of which 1 were waited for; matrix products, arithmetic and copies ran while one was open for 0% of the time, Pallas kernels for 7%

commit v1 on v0

--- a/solution.py
+++ b/solution.py
@@ -20,7 +20,7 @@
 TILES = NX // 8
 PARAMS = pltpu.CompilerParams(vmem_limit_bytes=24 * 1024 * 1024)
 VMEM = pl.BlockSpec(memory_space=pltpu.VMEM)
-SMEM = pl.BlockSpec(memory_space=pltpu.SMEM)
+HBM = pl.BlockSpec(memory_space=pltpu.HBM)
 
 
 def shape(*dims):
@@ -32,17 +32,19 @@
     return index * lax.axis_size(axes[1]) + lax.axis_index(axes[1])
 
 
-def cell_terms(head, soil, alpha_ref, n_ref, ks_ref):
-    alpha = jnp.full(head.shape, alpha_ref[0], F32)
-    expo = jnp.full(head.shape, n_ref[0], F32)
-    ks = jnp.full(head.shape, ks_ref[0], F32)
+def cell_terms(head, soil, tables):
+    def entry_of(table, entry):
+        line = tables[table, entry : entry + 1, :]
+        if head.shape[1] == 256:
+            line = jnp.concatenate([line, line], axis=1)
+        return jnp.broadcast_to(line, head.shape)
+
+    picked = [entry_of(table, 0) for table in range(4)]
     for entry in range(1, SOILS):
         here = soil == entry
-        alpha = jnp.where(here, alpha_ref[entry], alpha)
-        expo = jnp.where(here, n_ref[entry], expo)
-        ks = jnp.where(here, ks_ref[entry], ks)
+        picked = [jnp.where(here, entry_of(t, entry), x) for t, x in enumerate(picked)]
+    alpha, expo, ks, power = picked
     depth = -head
-    power = 1.0 - 1.0 / expo
     scaled = expo * jnp.log(alpha * depth)
     inverse = jnp.exp(-scaled)
     total = 1.0 + inverse
@@ -77,76 +79,109 @@
     return lax.broadcasted_iota(jnp.int32, dims, len(dims) - 2)
 
 
-def gather_sides(plane, z, odd_x, odd_y, packed):
+def gather_columns(plane, z, first_at, last_at, packed):
+    lane = lane_index((8, 128))
+    for tile in range(TILES):
+        rows = slice(8 * tile, 8 * tile + 8)
+        first = jnp.broadcast_to(plane[rows, 0:1], (8, 128))
+        last = jnp.broadcast_to(plane[rows, NY - 1 : NY], (8, 128))
+        packed = jnp.where(lane == TILES * z + tile + first_at, first, packed)
+        packed = jnp.where(lane == TILES * z + tile + last_at, last, packed)
+    return packed
+
+
+def gather_rows(plane, odd_x):
     low, high = plane[0:1, :], plane[NX - 1 : NX, :]
-    row_a = jnp.where(odd_x, low, high)
-    row_b = jnp.where(odd_x, high, low)
-    col_lane = lane_index((8, 128))
-    left, right = plane[:, 0:128], plane[:, 128:256]
+    return jnp.where(odd_x, low, high), jnp.where(odd_x, high, low)
+
+
+def spread_sides(z, odd_x, odd_y, row_a, row_b, packed):
+    low, high = jnp.where(odd_x, row_a, row_b), jnp.where(odd_x, row_b, row_a)
+    first = jnp.where(odd_y, packed, pltpu.roll(packed, 64, axis=1))
+    lane, row = lane_index((8, 128)), row_index((8, NY))
+    pieces = []
     for tile in range(TILES):
-        first = jnp.broadcast_to(left[8 * tile : 8 * tile + 8, 0:1], (8, 128))
-        last = jnp.broadcast_to(right[8 * tile : 8 * tile + 8, 127:128], (8, 128))
-        col_a = jnp.where(odd_y, first, last)
-        col_b = jnp.where(odd_y, last, first)
-        packed = jnp.where(col_lane == TILES * z + tile, col_a, packed)
-        packed = jnp.where(col_lane == TILES * z + tile + 64, col_b, packed)
-    return row_a, row_b, packed
-
-
-def spread_sides(z, odd_x, odd_y, rows_a, rows_b, packed):
-    row = row_index((NX, NY))
-    at_a = jnp.where(odd_x, 0, NX - 1)
-    at_b = jnp.where(odd_x, NX - 1, 0)
-    total = jnp.where(row == at_a, rows_a, 0.0) + jnp.where(row == at_b, rows_b, 0.0)
-    turned = pltpu.roll(packed, 128 - TILES * z, axis=1)
-    pieces = []
-    lane = lane_index((8, 128))
-    at_first = jnp.where(lane == 0, 1.0, 0.0)
-    at_last = jnp.where(lane == 127, 1.0, 0.0)
-    for tile in range(TILES):
-        col_a = jnp.broadcast_to(turned[:, tile : tile + 1], (8, 128))
-        col_b = jnp.broadcast_to(turned[:, tile + 64 : tile + 65], (8, 128))
-        first = jnp.where(odd_y, col_a, col_b)
-        last = jnp.where(odd_y, col_b, col_a)
-        pieces.append(jnp.concatenate([first * at_first, last * at_last], axis=1))
-    return total + jnp.concatenate(pieces, axis=0)
+        at = TILES * z + tile
+        left = jnp.broadcast_to(first[:, at : at + 1], (8, 128))
+        right = jnp.broadcast_to(first[:, at + 64 : at + 65], (8, 128))
+        left, right = jnp.where(lane == 0, left, 0.0), jnp.where(lane == 127, right, 0.0)
+        piece = jnp.concatenate([left, right], axis=1)
+        if tile == 0:
+            piece = piece + jnp.where(row == 0, low, 0.0)
+        if tile == TILES - 1:
+            piece = piece + jnp.where(row == 7, high, 0.0)
+        pieces.append(piece)
+    return jnp.concatenate(pieces, axis=0)
 
 
 def odd_sides():
     return (lax.axis_index("gx_1") % 2) == 1, lax.axis_index("gy_1") == 1
 
 
-def pack_kernel(head, soil, rhs, z_out, xa_out, xb_out, y_out):
+def column_lanes(odd_y):
+    return jnp.where(odd_y, 0, 64), jnp.where(odd_y, 64, 0)
+
+
+def pack_kernel(
+    head, soil, boundary, rhs, alpha, expo, ks,
+    head_out, soil_out, boundary_out, rhs_out, tables, z_out, xa_out, xb_out, y_out,
+    alpha_in, expo_in, ks_in, arrived,
+):
+    pairs = (
+        (alpha, alpha_in), (expo, expo_in), (ks, ks_in),
+        (head, head_out), (soil, soil_out), (rhs, rhs_out), (boundary, boundary_out),
+    )
+    copies = [
+        pltpu.make_async_copy(source, target, arrived.at[i])
+        for i, (source, target) in enumerate(pairs)
+    ]
+    for copy in copies:
+        copy.start()
     odd_x, odd_y = odd_sides()
     edge = jnp.where(lax.axis_index("gz") == 0, NZ - 1, 0)
-    for slot, ref in enumerate((head, soil, rhs)):
+    first_at, last_at = column_lanes(odd_y)
+    row = row_index((8, 128))
+    lines = []
+    for copy, source in zip(copies[:3], (alpha_in, expo_in, ks_in), strict=True):
+        copy.wait()
+        line = jnp.full((8, 128), source[0], F32)
+        for entry in range(1, SOILS):
+            line = jnp.where(row == entry, source[entry], line)
+        lines.append(line)
+    for slot, line in enumerate(lines + [1.0 - 1.0 / lines[1]]):
+        tables[slot] = line
+    for slot, (copy, ref) in enumerate(
+        zip(copies[3:6], (head_out, soil_out, rhs_out), strict=True)
+    ):
+        copy.wait()
         z_out[slot] = ref[edge].astype(F32)
-
-        def plane_step(z, packed):
-            row_a, row_b, packed = gather_sides(ref[z].astype(F32), z, odd_x, odd_y, packed)
-            xa_out[slot, pl.ds(z, 1), :] = row_a
-            xb_out[slot, pl.ds(z, 1), :] = row_b
-            return packed
-
-        y_out[slot] = lax.fori_loop(0, NZ, plane_step, jnp.zeros((8, 128), F32))
+        packed = jnp.zeros((8, 128), F32)
+        for z in range(NZ):
+            plane = ref[z].astype(F32)
+            packed = gather_columns(plane, z, first_at, last_at, packed)
+            row_a, row_b = gather_rows(plane, odd_x)
+            xa_out[slot, z : z + 1, :] = row_a
+            xb_out[slot, z : z + 1, :] = row_b
+        y_out[slot] = packed
+    copies[6].wait()
 
 
 def terms_kernel(
-    head, soil, rhs, xa, xb, y, alpha, expo, ks, coeffs, image, own_z, own_x, own_y, cond, dcond
+    head, soil, rhs, xa, xb, y, tables, coeffs, image, own_z, own_x, own_y, cond, dcond
 ):
     edge = jnp.where(lax.axis_index("gz") == 0, NZ - 1, 0)
 
     def terms_step(z, carry):
-        k, dk, capacity = cell_terms(head[z], soil[z], alpha, expo, ks)
+        k, dk, capacity = cell_terms(head[z], soil[z], tables)
         cond[z], dcond[z], coeffs[0, z] = k, dk, capacity
         return carry
 
     lax.fori_loop(0, NZ, terms_step, 0)
     own_z[0], own_z[1] = cond[edge], dcond[edge]
     for slot, side in enumerate((xa, xb)):
-        k, dk, _ = cell_terms(side[0], side[1].astype(jnp.int32), alpha, expo, ks)
+        k, dk, _ = cell_terms(side[0], side[1].astype(jnp.int32), tables)
         own_x[slot, 0], own_x[slot, 1] = k, dk
-    k, dk, _ = cell_terms(y[0], y[1].astype(jnp.int32), alpha, expo, ks)
+    k, dk, _ = cell_terms(y[0], y[1].astype(jnp.int32), tables)
     own_y[0], own_y[1] = k, dk
 
     row, lane = row_index((NX, NY)), lane_index((NX, NY))
@@ -195,7 +230,7 @@
 
 def first_kernel(
     head, boundary, rhs, interior, z_own, xa_own, xb_own, y_own, own_z, own_x, own_y,
-    z_far, xa_far, xb_far, ya_far, yb_far, alpha, expo, ks,
+    z_far, xa_far, xb_far, ya_far, yb_far, tables,
     image, z_out, xa_out, xb_out, y_out, face_z, face_x, face_y,
 ):
     odd_x, odd_y = odd_sides()
@@ -208,7 +243,7 @@
 
     def face(own, own_terms, far, there, slant):
         far_head = far[0] if there is None else jnp.where(there, far[0], -1.0)
-        k, dk, _ = cell_terms(far_head, far[1].astype(jnp.int32), alpha, expo, ks)
+        k, dk, _ = cell_terms(far_head, far[1].astype(jnp.int32), tables)
         near, away = couplings(own_terms[0], own_terms[1], own[0], k, dk, far_head, slant)
         if there is not None:
             near, away = jnp.where(there, near, 0.0), jnp.where(there, away, 0.0)
@@ -226,22 +261,22 @@
         sums_x.append(total)
     near, away, sum_z = face(z_own, (own_z[0], own_z[1]), z_far, None, tilt)
     face_z[0], face_z[1] = near, away
-    xa_out[...], xb_out[...] = sums_x
     image[...] = interior[...]
     image[edge] = image[edge] + sum_z
 
-    def plane_step(z, packed):
+    first_at, last_at = column_lanes(odd_y)
+    packed = jnp.zeros((8, 128), F32)
+    for z in range(NZ):
         total = image[z] + spread_sides(
-            z, odd_x, odd_y, xa_out[pl.ds(z, 1), :], xb_out[pl.ds(z, 1), :], sum_y
+            z, odd_x, odd_y, sums_x[0][z : z + 1, :], sums_x[1][z : z + 1, :], sum_y
         )
         plane = jnp.where(boundary[z] == 1, rhs[z], total)
         image[z] = plane
-        row_a, row_b, packed = gather_sides(plane, z, odd_x, odd_y, packed)
-        xa_out[pl.ds(z, 1), :] = row_a
-        xb_out[pl.ds(z, 1), :] = row_b
-        return packed
-
-    y_out[...] = lax.fori_loop(0, NZ, plane_step, jnp.zeros((8, 128), F32))
+        row_a, row_b = gather_rows(plane, odd_x)
+        xa_out[z : z + 1, :] = row_a
+        xb_out[z : z + 1, :] = row_b
+        packed = gather_columns(plane, z, first_at, last_at, packed)
+    y_out[...] = packed
     z_out[...] = image[edge]
 
 
@@ -274,30 +309,29 @@
 def second_kernel(
     boundary, rhs, v_ref, interior, partial, z_own, xa_own, xb_own, y_own,
     z_far, xa_far, xb_far, ya_far, yb_far, face_z, face_x, face_y,
-    image, sums_out, xa_sum, xb_sum,
+    image, sums_out,
 ):
     odd_x, odd_y = odd_sides()
     edge = jnp.where(lax.axis_index("gz") == 0, NZ - 1, 0)
     sum_y = face_y[0] * y_own[...] + face_y[1] * pick_y(ya_far[...], yb_far[...])
-    xa_sum[...] = face_x[0, 0] * xa_own[...] + face_x[0, 1] * xa_far[...]
-    xb_sum[...] = face_x[1, 0] * xb_own[...] + face_x[1, 1] * xb_far[...]
+    sum_xa = face_x[0, 0] * xa_own[...] + face_x[0, 1] * xa_far[...]
+    sum_xb = face_x[1, 0] * xb_own[...] + face_x[1, 1] * xb_far[...]
     image[...] = interior[...]
     image[edge] = image[edge] + face_z[0] * z_own[...] + face_z[1] * z_far[...]
 
-    def plane_step(z, sums):
+    sums = None
+    for z in range(NZ):
         v = v_ref[z]
         total = image[z] + spread_sides(
-            z, odd_x, odd_y, xa_sum[pl.ds(z, 1), :], xb_sum[pl.ds(z, 1), :], sum_y
+            z, odd_x, odd_y, sum_xa[z : z + 1, :], sum_xb[z : z + 1, :], sum_y
         )
         plane = jnp.where(boundary[z] == 1, v, total)
         image[z] = plane
-        products = (plane * rhs[z], plane * v, plane * plane)
-        return tuple(s + fold(p) for s, p in zip(sums, products, strict=True))
-
-    sums = lax.fori_loop(0, NZ, plane_step, (jnp.zeros((8, 128), F32),) * 3)
+        products = [fold(p) for p in (plane * rhs[z], plane * v, plane * plane)]
+        sums = products if z == 0 else [s + p for s, p in zip(sums, products, strict=True)]
     lane = lane_index((1, 8))
     row = jnp.zeros((1, 8), F32)
-    for slot, part in enumerate((partial[0], partial[1], partial[2]) + sums):
+    for slot, part in enumerate([partial[0], partial[1], partial[2]] + sums):
         value = jnp.sum(jnp.sum(part, axis=0, keepdims=True), axis=1, keepdims=True)
         row = jnp.where(lane == slot, value, row)
     sums_out[...] = jnp.broadcast_to(row, sums_out.shape)
@@ -331,7 +365,7 @@
     return solved
 
 
-def combine_kernel(rhs, first, second, sums, update, residual):
+def combine_kernel(rhs, first, second, sums, update_out, residual_out, update, residual, left):
     total = jnp.sum(sums[...], axis=0, keepdims=True)
     g00, g01, g11, g02, g12, g22 = (total[:, i : i + 1] for i in range(6))
     square = g00 + EPS
@@ -358,9 +392,15 @@
         a, b, c = rhs[z], first[z], second[z]
         update[z] = base * a + step * b
         residual[z] = a - (base * b + step * c)
+        for slot, (source, target) in enumerate(pairs):
+            pltpu.make_async_copy(source.at[z], target.at[z], left.at[slot, z]).start()
         return carry
 
+    pairs = ((update, update_out), (residual, residual_out))
     lax.fori_loop(0, NZ, plane_step, 0)
+    for z in range(NZ):
+        for slot, (source, target) in enumerate(pairs):
+            pltpu.make_async_copy(source.at[z], target.at[z], left.at[slot, z]).wait()
 
 
 def cost(flops):
@@ -368,7 +408,7 @@
 
 
 def swap(x, axis, start, count):
-    pairs = [(i, i + 1) for i in range(start, count - 1, 2)]
+    pairs = [(i, (i + 1) % count) for i in range(start, count, 2)]
     return lax.ppermute(x, axis, pairs + [(b, a) for a, b in pairs])
 
 
@@ -383,12 +423,12 @@
     )
 
 
-def call(kernel, ins, outs, flops, scratch=()):
+def call(kernel, ins, outs, flops, out_specs=None, scratch=()):
     return pl.pallas_call(
         kernel,
         out_shape=outs,
         in_specs=ins,
-        out_specs=jax.tree.map(lambda _: VMEM, outs),
+        out_specs=out_specs or tuple(VMEM for _ in outs),
         scratch_shapes=list(scratch),
         compiler_params=PARAMS,
         cost_estimate=cost(flops),
@@ -397,40 +437,47 @@
 
 
 def body(head, soil, boundary, rhs, soil_alpha, soil_n, soil_ks):
-    tables = (soil_alpha, soil_n, soil_ks)
+    whole = shape(*BLOCK)
+    counts = jax.ShapeDtypeStruct(BLOCK, jnp.int32)
     sides = (shape(3, NX, NY), shape(3, 8, NY), shape(3, 8, NY), shape(3, 8, 128))
-    z, xa, xb, y = call(pack_kernel, [VMEM] * 3, sides, 1000000)(head, soil, rhs)
+    sources = (head, soil, boundary, rhs, soil_alpha, soil_n, soil_ks)
+    sources = [pltpu.with_memory_space_constraint(x, pltpu.HBM) for x in sources]
+    head, soil, boundary, rhs, tables, z, xa, xb, y = call(
+        pack_kernel,
+        [HBM] * 7,
+        (whole, counts, counts, whole, shape(4, 8, 128)) + sides,
+        1000000,
+        scratch=[pltpu.SMEM((SOILS,), F32)] * 3 + [pltpu.SemaphoreType.DMA((7,))],
+    )(*sources)
     far = exchange(z, xa, xb, y)
     own = (shape(2, NX, NY), shape(2, 2, 8, NY), shape(2, 8, 128))
     coeffs, interior, own_z, own_x, own_y = call(
         terms_kernel,
-        [VMEM] * 6 + [SMEM] * 3,
-        (shape(7, *BLOCK), shape(*BLOCK)) + own,
+        [VMEM] * 7,
+        (shape(7, *BLOCK), whole) + own,
         40000000,
-        (pltpu.VMEM(BLOCK, F32), pltpu.VMEM(BLOCK, F32)),
-    )(head, soil, rhs, xa, xb, y, *tables)
+        scratch=[pltpu.VMEM(BLOCK, F32)] * 2,
+    )(head, soil, rhs, xa, xb, y, tables)
     sides = (shape(NX, NY), shape(8, NY), shape(8, NY), shape(8, 128))
     first, z1, xa1, xb1, y1, face_z, face_x, face_y = call(
-        first_kernel,
-        [VMEM] * 16 + [SMEM] * 3,
-        (shape(*BLOCK),) + sides + own,
-        8000000,
-    )(head, boundary, rhs, interior, z, xa, xb, y, own_z, own_x, own_y, *far, *tables)
+        first_kernel, [VMEM] * 17, (whole,) + sides + own, 8000000
+    )(head, boundary, rhs, interior, z, xa, xb, y, own_z, own_x, own_y, *far, tables)
     far = exchange(z1, xa1, xb1, y1)
-    interior, partial = call(
-        inner_kernel, [VMEM] * 3, (shape(*BLOCK), shape(3, 8, 128)), 8000000
-    )(coeffs, first, rhs)
-    second, sums = call(
-        second_kernel,
-        [VMEM] * 17,
-        (shape(*BLOCK), shape(256, 8)),
-        8000000,
-        (pltpu.VMEM((8, NY), F32), pltpu.VMEM((8, NY), F32)),
-    )(boundary, rhs, first, interior, partial, z1, xa1, xb1, y1, *far, face_z, face_x, face_y)
+    interior, partial = call(inner_kernel, [VMEM] * 3, (whole, shape(3, 8, 128)), 8000000)(
+        coeffs, first, rhs
+    )
+    second, sums = call(second_kernel, [VMEM] * 17, (whole, shape(256, 8)), 8000000)(
+        boundary, rhs, first, interior, partial, z1, xa1, xb1, y1, *far, face_z, face_x, face_y
+    )
     sums = lax.all_to_all(sums, AXES, 0, 0)
-    return call(combine_kernel, [VMEM] * 4, (shape(*BLOCK), shape(*BLOCK)), 1000000)(
-        rhs, first, second, sums
-    )
+    return call(
+        combine_kernel,
+        [VMEM] * 4,
+        (whole, whole),
+        1000000,
+        (HBM, HBM),
+        [pltpu.VMEM(BLOCK, F32)] * 2 + [pltpu.SemaphoreType.DMA((2, NZ))],
+    )(rhs, first, second, sums)
 
 
 def solution(mesh):

time: 71.2 us -> 52.8 us (0.74)
  local copies, waits for them, and re-layouts: 7.16 us -> 0 us
  blocking collectives: 26.9 us -> 22.7 us
  Pallas kernels: 13.7 us -> 9.94 us
  starting transfers between devices: 21.9 us -> 18.4 us
    unnamed x20 -> x0, local copies, waits for them, and re-layouts: 7.16 us -> none
    all_to_all x1, blocking collectives: 26.9 us -> 22.7 us  [body(): sums = lax.all_to_all(sums, AXES, 0, 0)]
    pallas_call x6, Pallas kernels: 13.7 us -> 9.94 us  [the longest x1 3.74 us: body(): call(terms_kernel, [VMEM] * 7, (shape(7, *BLOCK), whole) + own, 40000000,...]
    ppermute x10, starting transfers between devices: 21.9 us -> 18.4 us  [swap(): return lax.ppermute(x, axis, pairs + [(b, a) for a, b in pairs])]
  transfers between devices with their start and end apart: 10 -> 10, of which waited for: 1 -> 2; matrix products, arithmetic and copies ran while one was open for 0% -> 0% of each run, Pallas kernels for 7% -> 9%
where the time goes in v1:
time: 52.8 us; the launch traced here: 52.7 us
  blocking collectives  22.7 us (43%)
  starting transfers between devices  18.4 us (35%)
  Pallas kernels  9.94 us (19%)
  waiting for transfers between devices  0.88 us (2%)
  between operations  0.72 us (1%)
    all_to_all x1, blocking collectives, body(): sums = lax.all_to_all(sums, AXES, 0, 0)  22.7 us
    ppermute x10, starting transfers between devices, swap(): return lax.ppermute(x, axis, pairs + [(b, a) for a, b in pairs])  18.4 us
    pallas_call x1, Pallas kernels, body(): call(terms_kernel, [VMEM] * 7, (shape(7, *BLOCK), whole) + own, 40000000,...  3.74 us
    pallas_call x1, Pallas kernels, body(): call(combine_kernel, [VMEM] * 4, (whole, whole), 1000000, (HBM, HBM), [pl...  2.18 us
    pallas_call x1, Pallas kernels, body(): call(pack_kernel, [HBM] * 7, (whole, counts, counts, whole, shape(4, 8, 1...  1.73 us
  transfers between devices with their start and end apart: 10, of which 2 were waited for; matrix products, arithmetic and copies ran while one was open for 0% of the time, Pallas kernels for 9%

profile of v1, /device:TPU:1, one launch (start us, length us, event | category | flops | bytes accessed | tf_op | source)
XLA Modules:
  0.0 52.7 jit_solution(11572805750805225159)
XLA Ops:
  0.6 1.7 %pack_kernel.1 = (f32[8,64,256]{2,1,0:T(8,128)S(1)}, s32[8,64,256]{2,1,0:T(8,128)S(1)}, s32[8,64,256]{2,1,0:T(8,128)S(1)}, f32[8,64,256]{2,1,0:T(8,128)S(1)}, f3...) custom-call(f32[8,64,256]{2,1,0:T(8,128)} %head.1, ...), custom_call_target="tpu_custom_call" | custom-call | flops 1000000 | bytes 4194304 | tf_op jit(solution)/shard_map/pack_kernel/pallas_call | solution.py:445
  2.4 2.5 %collective-permute-start = (f32[3,64,256]{2,1,0:T(8,128)S(1)}, f32[3,64,256]{2,1,0:T(8,128)S(1)}, u32[]{:S(2)}, u32[]{:S(2)}) collective-permute-start(f32[3,64,256]{2,1,0:T(8,128)S(1)} %get-tuple-element.37.z_own), channel_id=1, source_target_pairs={{0,1},{1,0},{2,3},{3,2},{4,5},{5,4},{6,7},{7,6},{8,9},{9,8},{10,11... | collective-permute-start | bytes 589832 | tf_op jit(solution)/shard_map/ppermute | solution.py:412
  4.9 1.2 %collective-permute-start.1 = (f32[3,8,256]{2,1,0:T(8,128)S(1)}, f32[3,8,256]{2,1,0:T(8,128)S(1)}, u32[]{:S(2)}, u32[]{:S(2)}) collective-permute-start(f32[3,8,256]{2,1,0:T(8,128)S(1)} %get-tuple-element.32.xa.xa_own), channel_id=1, source_target_pairs={{0,16},{32,48},{64,80},{96,112},{128,144},{160,176},{192,208},{224... | collective-permute-start | bytes 73736 | tf_op jit(solution)/shard_map/ppermute | solution.py:412
  6.1 4.3 %collective-permute-start.2 = (f32[3,8,256]{2,1,0:T(8,128)S(1)}, f32[3,8,256]{2,1,0:T(8,128)S(1)}, u32[]{:S(2)}, u32[]{:S(2)}) collective-permute-start(f32[3,8,256]{2,1,0:T(8,128)S(1)} %get-tuple-element.33.xb.xb_own), channel_id=1, source_target_pairs={{16,32},{48,64},{80,96},{112,128},{144,160},{176,192},{208,224},{2... | collective-permute-start | bytes 73736 | tf_op jit(solution)/shard_map/ppermute | solution.py:412
  10.4 4.4 %collective-permute-start.4 = (f32[3,8,128]{2,1,0:T(8,128)S(1)}, f32[3,8,128]{2,1,0:T(8,128)S(1)}, u32[]{:S(2)}, u32[]{:S(2)}) collective-permute-start(f32[3,8,128]{2,1,0:T(8,128)S(1)} %get-tuple-element.34.y.y_own), channel_id=1, source_target_pairs={{2,4},{6,8},{10,12},{14,0},{4,2},{8,6},{12,10},{0,14},{3,5},{7,9},... | collective-permute-start | bytes 36872 | tf_op jit(solution)/shard_map/ppermute | solution.py:412
  14.8 1.1 %collective-permute-start.3 = (f32[3,8,128]{2,1,0:T(8,128)S(1)}, f32[3,8,128]{2,1,0:T(8,128)S(1)}, u32[]{:S(2)}, u32[]{:S(2)}) collective-permute-start(f32[3,8,128]{2,1,0:T(8,128)S(1)} %get-tuple-element.34.y.y_own), channel_id=1, source_target_pairs={{0,2},{4,6},{8,10},{12,14},{2,0},{6,4},{10,8},{14,12},{1,3},{5,7},... | collective-permute-start | bytes 36872 | tf_op jit(solution)/shard_map/ppermute | solution.py:412
  15.9 3.7 %terms_kernel.1 = (f32[7,8,64,256]{3,2,1,0:T(8,128)S(1)}, f32[8,64,256]{2,1,0:T(8,128)S(1)}, f32[2,64,256]{2,1,0:T(8,128)S(1)}, f32[2,2,8,256]{3,2,1,0:T(8,128)S(1)}, f32[2,8,128]{2,1,0:T(8,128)S(1)}) custom-call(f32[8,64,256]{2,1,0:T(8,128)S(1)} %get-tuple-element.29.head, s32[8,64,256]{2,1,0:T(8,128)S(1)} %get-tuple-element.31.soil, ...), custom_call_target="tpu_custom_call" | custom-call | flops 40000000 | bytes 4194304 | tf_op jit(solution)/shard_map/terms_kernel/pallas_call | solution.py:454
  19.7 0.0 collective-permute-done.4.yb_far
  19.7 0.0 collective-permute-done.3.ya_far
  19.7 0.0 collective-permute-done.1.xa_far
  19.7 0.0 collective-permute-done.2.xb_far
  19.7 0.0 collective-permute-done.z_far
  19.7 0.9 %first_kernel.1 = (f32[8,64,256]{2,1,0:T(8,128)S(1)}, f32[64,256]{1,0:T(8,128)S(1)}, f32[8,256]{1,0:T(8,128)S(1)}, f32[8,256]{1,0:T(8,128)S(1)}, f32[8,128]{1,0:...) custom-call(f32[8,64,256]{2,1,0:T(8,128)S(1)} %get-tuple-element.29.head, ...), custom_call_target="tpu_custom_call" | custom-call | flops 8000000 | bytes 4194304 | tf_op jit(solution)/shard_map/first_kernel/pallas_call | solution.py:462
  20.6 0.8 %collective-permute-start.5 = (f32[64,256]{1,0:T(8,128)S(1)}, f32[64,256]{1,0:T(8,128)S(1)}, u32[]{:S(2)}, u32[]{:S(2)}) collective-permute-start(f32[64,256]{1,0:T(8,128)S(1)} %get-tuple-element.45.z_own), channel_id=1, source_target_pairs={{0,1},{1,0},{2,3},{3,2},{4,5},{5,4},{6,7},{7,6},{8,9},{9,8},{10,11... | collective-permute-start | bytes 196616 | tf_op jit(solution)/shard_map/ppermute | solution.py:412
  21.4 0.0 collective-permute-start.6
  21.4 0.9 %collective-permute-start.7 = (f32[8,256]{1,0:T(8,128)S(1)}, f32[8,256]{1,0:T(8,128)S(1)}, u32[]{:S(2)}, u32[]{:S(2)}) collective-permute-start(f32[8,256]{1,0:T(8,128)S(1)} %get-tuple-element.47.xb_own), channel_id=1, source_target_pairs={{16,32},{48,64},{80,96},{112,128},{144,160},{176,192},{208,224},{2... | collective-permute-start | bytes 24584 | tf_op jit(solution)/shard_map/ppermute | solution.py:412
  22.3 3.1 %collective-permute-start.9 = (f32[8,128]{1,0:T(8,128)S(1)}, f32[8,128]{1,0:T(8,128)S(1)}, u32[]{:S(2)}, u32[]{:S(2)}) collective-permute-start(f32[8,128]{1,0:T(8,128)S(1)} %get-tuple-element.48.y_own), channel_id=1, source_target_pairs={{2,4},{6,8},{10,12},{14,0},{4,2},{8,6},{12,10},{0,14},{3,5},{7,9},... | collective-permute-start | bytes 12296 | tf_op jit(solution)/shard_map/ppermute | solution.py:412
  25.5 0.0 collective-permute-start.8
  25.5 0.9 %inner_kernel.1 = (f32[8,64,256]{2,1,0:T(8,128)S(1)}, f32[3,8,128]{2,1,0:T(8,128)S(1)}) custom-call(f32[7,8,64,256]{3,2,1,0:T(8,128)S(1)} %get-tuple-element.42.coeffs, f32[8,64,256]{2,1,0:T(8,128)S(1)} %get-tuple-element.41.v_ref.first, f32[8,64,256]{2,1,0:T(8,128)S(1)} %get-tuple-element.28.rhs), custom_call_target="tpu_custom_call" | custom-call | flops 8000000 | bytes 4194304 | tf_op jit(solution)/shard_map/inner_kernel/pallas_call | solution.py:466
  26.4 0.4 collective-permute-done.9.yb_far
  26.8 0.0 collective-permute-done.8.ya_far
  26.8 0.0 collective-permute-done.6.xa_far
  26.8 0.5 collective-permute-done.7.xb_far
  27.2 0.0 collective-permute-done.5.z_far
  27.3 0.5 second_kernel.1
  27.8 22.7 %all_to_all.11 = f32[256,1,8]{2,1,0:T(1,128)S(1)} all-to-all(f32[256,1,8]{2,1,0:T(1,128)S(1)} %bitcast.5), channel_id=1, replica_groups=mesh['gx_0'=4,'gx_1'=4,'gy_0'=4,'gy_1'=2,'gz'=2] {'gx_0','gx_1','gy_0','..., dimensions={0} | all-to-all | bytes 16384 | tf_op jit(solution)/shard_map/all_to_all | solution.py:472
  50.5 2.2 %combine_kernel.1 = (f32[8,64,256]{2,1,0:T(8,128)}, f32[8,64,256]{2,1,0:T(8,128)}) custom-call(f32[8,64,256]{2,1,0:T(8,128)S(1)} %get-tuple-element.28.rhs, f32[8,64,256]{2,1,0:T(8,128)S(1)} %get-tuple-element.41.v_ref.first, f32[8,64,256]{2,1,0:T(8,128)S(1)} %get-tuple-element.52.second, f32[256,8]{1,0:T(8,128)S(1)} %bitcast.4), custom_call_target="tpu_custom_call" | custom-call | flops 1000000 | bytes 4194304 | tf_op jit(solution)/shard_map/combine_kernel/pallas_call | solution.py:473
Async XLA Ops:
  2.4 17.3 %collective-permute-start = (f32[3,64,256]{2,1,0:T(8,128)S(1)}, f32[3,64,256]{2,1,0:T(8,128)S(1)}, u32[]{:S(2)}, u32[]{:S(2)}) collective-permute-start(f32[3,64,256]{2,1,0:T(8,128)S(1)} %get-tuple-element.37.z_own), channel_id=1, source_target_pairs={{0,1},{1,0},{2,3},{3,2},{4,5},{5,4},{6,7},{7,6},{8,9},{9,8},{10,11... | collective-permute-start | bytes 589832 | tf_op jit(solution)/shard_map/ppermute | solution.py:412
  4.9 14.8 %collective-permute-start.1 = (f32[3,8,256]{2,1,0:T(8,128)S(1)}, f32[3,8,256]{2,1,0:T(8,128)S(1)}, u32[]{:S(2)}, u32[]{:S(2)}) collective-permute-start(f32[3,8,256]{2,1,0:T(8,128)S(1)} %get-tuple-element.32.xa.xa_own), channel_id=1, source_target_pairs={{0,16},{32,48},{64,80},{96,112},{128,144},{160,176},{192,208},{224... | collective-permute-start | bytes 73736 | tf_op jit(solution)/shard_map/ppermute | solution.py:412
  6.1 13.6 %collective-permute-start.2 = (f32[3,8,256]{2,1,0:T(8,128)S(1)}, f32[3,8,256]{2,1,0:T(8,128)S(1)}, u32[]{:S(2)}, u32[]{:S(2)}) collective-permute-start(f32[3,8,256]{2,1,0:T(8,128)S(1)} %get-tuple-element.33.xb.xb_own), channel_id=1, source_target_pairs={{16,32},{48,64},{80,96},{112,128},{144,160},{176,192},{208,224},{2... | collective-permute-start | bytes 73736 | tf_op jit(solution)/shard_map/ppermute | solution.py:412
  10.4 9.3 %collective-permute-start.4 = (f32[3,8,128]{2,1,0:T(8,128)S(1)}, f32[3,8,128]{2,1,0:T(8,128)S(1)}, u32[]{:S(2)}, u32[]{:S(2)}) collective-permute-start(f32[3,8,128]{2,1,0:T(8,128)S(1)} %get-tuple-element.34.y.y_own), channel_id=1, source_target_pairs={{2,4},{6,8},{10,12},{14,0},{4,2},{8,6},{12,10},{0,14},{3,5},{7,9},... | collective-permute-start | bytes 36872 | tf_op jit(solution)/shard_map/ppermute | solution.py:412
  14.8 4.9 %collective-permute-start.3 = (f32[3,8,128]{2,1,0:T(8,128)S(1)}, f32[3,8,128]{2,1,0:T(8,128)S(1)}, u32[]{:S(2)}, u32[]{:S(2)}) collective-permute-start(f32[3,8,128]{2,1,0:T(8,128)S(1)} %get-tuple-element.34.y.y_own), channel_id=1, source_target_pairs={{0,2},{4,6},{8,10},{12,14},{2,0},{6,4},{10,8},{14,12},{1,3},{5,7},... | collective-permute-start | bytes 36872 | tf_op jit(solution)/shard_map/ppermute | solution.py:412
  20.6 6.6 %collective-permute-start.5 = (f32[64,256]{1,0:T(8,128)S(1)}, f32[64,256]{1,0:T(8,128)S(1)}, u32[]{:S(2)}, u32[]{:S(2)}) collective-permute-start(f32[64,256]{1,0:T(8,128)S(1)} %get-tuple-element.45.z_own), channel_id=1, source_target_pairs={{0,1},{1,0},{2,3},{3,2},{4,5},{5,4},{6,7},{7,6},{8,9},{9,8},{10,11... | collective-permute-start | bytes 196616 | tf_op jit(solution)/shard_map/ppermute | solution.py:412
  21.4 5.3 %collective-permute-start.6 = (f32[8,256]{1,0:T(8,128)S(1)}, f32[8,256]{1,0:T(8,128)S(1)}, u32[]{:S(2)}, u32[]{:S(2)}) collective-permute-start(f32[8,256]{1,0:T(8,128)S(1)} %get-tuple-element.46.xa_own), channel_id=1, source_target_pairs={{0,16},{32,48},{64,80},{96,112},{128,144},{160,176},{192,208},{224... | collective-permute-start | bytes 24584 | tf_op jit(solution)/shard_map/ppermute | solution.py:412
  21.4 5.8 %collective-permute-start.7 = (f32[8,256]{1,0:T(8,128)S(1)}, f32[8,256]{1,0:T(8,128)S(1)}, u32[]{:S(2)}, u32[]{:S(2)}) collective-permute-start(f32[8,256]{1,0:T(8,128)S(1)} %get-tuple-element.47.xb_own), channel_id=1, source_target_pairs={{16,32},{48,64},{80,96},{112,128},{144,160},{176,192},{208,224},{2... | collective-permute-start | bytes 24584 | tf_op jit(solution)/shard_map/ppermute | solution.py:412
  22.3 4.4 %collective-permute-start.9 = (f32[8,128]{1,0:T(8,128)S(1)}, f32[8,128]{1,0:T(8,128)S(1)}, u32[]{:S(2)}, u32[]{:S(2)}) collective-permute-start(f32[8,128]{1,0:T(8,128)S(1)} %get-tuple-element.48.y_own), channel_id=1, source_target_pairs={{2,4},{6,8},{10,12},{14,0},{4,2},{8,6},{12,10},{0,14},{3,5},{7,9},... | collective-permute-start | bytes 12296 | tf_op jit(solution)/shard_map/ppermute | solution.py:412
  25.5 1.3 %collective-permute-start.8 = (f32[8,128]{1,0:T(8,128)S(1)}, f32[8,128]{1,0:T(8,128)S(1)}, u32[]{:S(2)}, u32[]{:S(2)}) collective-permute-start(f32[8,128]{1,0:T(8,128)S(1)} %get-tuple-element.48.y_own), channel_id=1, source_target_pairs={{0,2},{4,6},{8,10},{12,14},{2,0},{6,4},{10,8},{14,12},{1,3},{5,7},... | collective-permute-start | bytes 12296 | tf_op jit(solution)/shard_map/ppermute | solution.py:412

commit v2 on v1

--- a/solution.py
+++ b/solution.py
@@ -5,6 +5,7 @@
 from jax.experimental.pallas import tpu as pltpu
 from jax.sharding import Mesh
 from jax.sharding import PartitionSpec as P
+
 
 AXES = ("gx_0", "gx_1", "gy_0", "gy_1", "gz")
 GX = ("gx_0", "gx_1")
@@ -15,6 +16,7 @@
 PORE = 0.4
 STEP = 0.25
 F32 = jnp.float32
+LOG2E = 1.4426950408889634
 NZ, NX, NY = 8, 64, 256
 BLOCK = (NZ, NX, NY)
 TILES = NX // 8
@@ -32,42 +34,48 @@
     return index * lax.axis_size(axes[1]) + lax.axis_index(axes[1])
 
 
+def pick(tables, soil):
+    rows = []
+    for row in range(0, soil.shape[0], 8):
+        tiles = []
+        for lane in range(0, soil.shape[1], 128):
+            index = soil[row : row + 8, lane : lane + 128]
+            tiles.append(
+                [
+                    jnp.take_along_axis(tables[t], index, axis=0, mode="promise_in_bounds")
+                    for t in range(4)
+                ]
+            )
+        rows.append([jnp.concatenate(x, axis=1) for x in zip(*tiles, strict=True)])
+    return [jnp.concatenate(x, axis=0) for x in zip(*rows, strict=True)]
+
+
 def cell_terms(head, soil, tables):
-    def entry_of(table, entry):
-        line = tables[table, entry : entry + 1, :]
-        if head.shape[1] == 256:
-            line = jnp.concatenate([line, line], axis=1)
-        return jnp.broadcast_to(line, head.shape)
-
-    picked = [entry_of(table, 0) for table in range(4)]
-    for entry in range(1, SOILS):
-        here = soil == entry
-        picked = [jnp.where(here, entry_of(t, entry), x) for t, x in enumerate(picked)]
-    alpha, expo, ks, power = picked
-    depth = -head
-    scaled = expo * jnp.log(alpha * depth)
-    inverse = jnp.exp(-scaled)
+    minus_alpha, expo, ks, minus_power = pick(tables, soil)
+    scaled = expo * jnp.log(minus_alpha * head)
+    inverse = jnp.exp2(-LOG2E * scaled)
     total = 1.0 + inverse
     part = jnp.log(total)
-    root = jnp.exp((-0.5 * power) * (part + scaled))
-    bent = jnp.exp(-power * part)
-    share = 1.0 / total
-    rise = (expo - 1.0) / depth
+    root = jnp.exp2(0.5 * (minus_power * (part + scaled)))
+    bent = jnp.exp2(minus_power * part)
+    rise = (1.0 - expo) / (head * total)
     gap = 1.0 - bent
-    sat = root * root
     conduct = ks * root * gap
-    cond = conduct * gap
-    dcond = conduct * rise * share * (0.5 * gap + 2.0 * bent * inverse)
-    capacity = sat * (SPEC / STEP + (PORE / STEP) * rise * share)
+    cond = 2.0 * (conduct * gap)
+    dcond = conduct * rise * (gap + 4.0 * (bent * inverse))
+    capacity = root * root * (SPEC / STEP + (PORE / STEP) * rise)
     return cond, dcond, capacity
 
 
 def couplings(k_own, dk_own, h_own, k_far, dk_far, h_far, tilt):
     part = 1.0 / (k_own + k_far)
     own, far = k_own * part, k_far * part
-    slope = h_own - h_far - tilt
-    near = 2.0 * far * (k_own + slope * far * dk_own)
-    away = -2.0 * own * (k_far - slope * own * dk_far)
+    slope = h_own - h_far
+    if tilt is not None:
+        slope = slope - tilt
+    mean = far * k_own
+    near = mean + far * far * (slope * dk_own)
+    away = own * own * (slope * dk_far) - mean
     return near, away
 
 
@@ -123,13 +131,13 @@
 
 
 def pack_kernel(
-    head, soil, boundary, rhs, alpha, expo, ks,
-    head_out, soil_out, boundary_out, rhs_out, tables, z_out, xa_out, xb_out, y_out,
+    head, soil, rhs, alpha, expo, ks,
+    head_out, soil_out, rhs_out, tables, z_out, xa_out, xb_out, y_out,
     alpha_in, expo_in, ks_in, arrived,
 ):
     pairs = (
         (alpha, alpha_in), (expo, expo_in), (ks, ks_in),
-        (head, head_out), (soil, soil_out), (rhs, rhs_out), (boundary, boundary_out),
+        (head, head_out), (soil, soil_out), (rhs, rhs_out),
     )
     copies = [
         pltpu.make_async_copy(source, target, arrived.at[i])
@@ -148,7 +156,8 @@
         for entry in range(1, SOILS):
             line = jnp.where(row == entry, source[entry], line)
         lines.append(line)
-    for slot, line in enumerate(lines + [1.0 - 1.0 / lines[1]]):
+    lines[0] = -lines[0]
+    for slot, line in enumerate(lines + [LOG2E / lines[1] - LOG2E]):
         tables[slot] = line
     for slot, (copy, ref) in enumerate(
         zip(copies[3:6], (head_out, soil_out, rhs_out), strict=True)
@@ -163,12 +172,30 @@
             xa_out[slot, z : z + 1, :] = row_a
             xb_out[slot, z : z + 1, :] = row_b
         y_out[slot] = packed
-    copies[6].wait()
+
+
+def end_rows(x):
+    tail = x[NX - 8 :, :]
+    tail = jnp.where(row_index(tail.shape) < 7, tail, 0.0)
+    return jnp.concatenate([x[: NX - 8, :], tail], axis=0)
+
+
+def end_lanes(x):
+    tail = x[:, NY - 128 :]
+    tail = jnp.where(lane_index(tail.shape) < 127, tail, 0.0)
+    return jnp.concatenate([x[:, : NY - 128], tail], axis=1)
+
+
+def up(x, axis):
+    return pltpu.roll(x, x.shape[axis] - 1, axis=axis)
 
 
 def terms_kernel(
-    head, soil, rhs, xa, xb, y, tables, coeffs, image, own_z, own_x, own_y, cond, dcond
+    head, soil, rhs, xa, xb, y, tables, boundary,
+    coeffs, image, own_z, own_x, own_y, boundary_out, cond, dcond, arrived,
 ):
+    copy = pltpu.make_async_copy(boundary, boundary_out, arrived)
+    copy.start()
     edge = jnp.where(lax.axis_index("gz") == 0, NZ - 1, 0)
 
     def terms_step(z, carry):
@@ -177,6 +204,8 @@
         return carry
 
     lax.fori_loop(0, NZ, terms_step, 0)
+    nothing = jnp.zeros((NX, NY), F32)
+    cond[NZ], dcond[NZ] = nothing, nothing
     own_z[0], own_z[1] = cond[edge], dcond[edge]
     for slot, side in enumerate((xa, xb)):
         k, dk, _ = cell_terms(side[0], side[1].astype(jnp.int32), tables)
@@ -184,44 +213,25 @@
     k, dk, _ = cell_terms(y[0], y[1].astype(jnp.int32), tables)
     own_y[0], own_y[1] = k, dk
 
-    row, lane = row_index((NX, NY)), lane_index((NX, NY))
-
-    def faces_step(z, carry):
-        below_near, below_away = carry
+    def faces_step(z, below):
         k, dk, h, v = cond[z], dcond[z], head[z], rhs[z]
         above = jnp.minimum(z + 1, NZ - 1)
-        under = jnp.maximum(z - 1, 0)
-        near, away = couplings(k, dk, h, cond[above], dcond[above], head[above], 1.0)
-        inner = jnp.where(z < NZ - 1, 1.0, 0.0)
-        near, away = near * inner, away * inner
-        diagonal = coeffs[0, z] + near - below_away
-        coeffs[1, z] = away
-        coeffs[2, z] = -below_near
-        total = away * rhs[above] - below_near * rhs[under]
-        carry = near, away
-        for slot, axis, position in ((3, 0, row), (5, 1, lane)):
-            size = k.shape[axis]
-
-            def up(x):
-                return pltpu.roll(x, size - 1, axis=axis)
-
-            def down(x):
-                return pltpu.roll(x, 1, axis=axis)
-
-            near, away = couplings(k, dk, h, up(k), up(dk), up(h), 0.0)
-            inside = position < size - 1
-            near, away = jnp.where(inside, near, 0.0), jnp.where(inside, away, 0.0)
-            past = -down(near)
-            diagonal = diagonal + near - down(away)
-            coeffs[slot, z] = away
-            coeffs[slot + 1, z] = past
-            total = total + away * up(v) + past * down(v)
-        coeffs[0, z] = diagonal
-        image[z] = total + diagonal * v
-        return carry
-
-    nothing = jnp.zeros((NX, NY), F32)
-    lax.fori_loop(0, NZ, faces_step, (nothing, nothing))
+        near, away = couplings(k, dk, h, cond[z + 1], dcond[z + 1], head[above], 1.0)
+        coeffs[1, z], coeffs[2, z] = near, away
+        flux = near * v + away * rhs[above]
+        total = coeffs[0, z] * v + flux - below
+        below = flux
+        for slot, axis, end in ((3, 0, end_rows), (5, 1, end_lanes)):
+            far = (end(up(k, axis)), end(up(dk, axis)), up(h, axis))
+            near, away = couplings(k, dk, h, *far, None)
+            coeffs[slot, z], coeffs[slot + 1, z] = near, away
+            flux = near * v + away * up(v, axis)
+            total = total + flux - pltpu.roll(flux, 1, axis=axis)
+        image[z] = total
+        return below
+
+    lax.fori_loop(0, NZ, faces_step, nothing)
+    copy.wait()
 
 
 def pick_y(y_a, y_b):
@@ -252,11 +262,11 @@
     lane = lane_index((8, 128))
     far_y = tuple(pick_y(ya_far[slot], yb_far[slot]) for slot in range(3))
     there_y = jnp.logical_or(lane < 64, has_y)
-    near, away, sum_y = face((y_own[0], None, y_own[2]), (own_y[0], own_y[1]), far_y, there_y, 0.0)
+    near, away, sum_y = face((y_own[0], None, y_own[2]), (own_y[0], own_y[1]), far_y, there_y, None)
     face_y[0], face_y[1] = near, away
     sums_x = []
     for slot, (own, far, there) in enumerate(((xa_own, xa_far, None), (xb_own, xb_far, has_x))):
-        near, away, total = face(own, (own_x[slot, 0], own_x[slot, 1]), far, there, 0.0)
+        near, away, total = face(own, (own_x[slot, 0], own_x[slot, 1]), far, there, None)
         face_x[slot, 0], face_x[slot, 1] = near, away
         sums_x.append(total)
     near, away, sum_z = face(z_own, (own_z[0], own_z[1]), z_far, None, tilt)
@@ -288,20 +298,22 @@
 
 
 def inner_kernel(coeffs, v_ref, rhs, interior, partial):
-    def plane_step(z, sums):
+    def plane_step(z, carry):
+        below, sums = carry
         v, start = v_ref[z], rhs[z]
         above = jnp.minimum(z + 1, NZ - 1)
-        under = jnp.maximum(z - 1, 0)
-        total = coeffs[0, z] * v + coeffs[1, z] * v_ref[above] + coeffs[2, z] * v_ref[under]
-        total = total + coeffs[3, z] * pltpu.roll(v, NX - 1, axis=0)
-        total = total + coeffs[4, z] * pltpu.roll(v, 1, axis=0)
-        total = total + coeffs[5, z] * pltpu.roll(v, NY - 1, axis=1)
-        total = total + coeffs[6, z] * pltpu.roll(v, 1, axis=1)
+        flux = coeffs[1, z] * v + coeffs[2, z] * v_ref[above]
+        total = coeffs[0, z] * v + flux - below
+        below = flux
+        for slot, axis in ((3, 0), (5, 1)):
+            flux = coeffs[slot, z] * v + coeffs[slot + 1, z] * up(v, axis)
+            total = total + flux - pltpu.roll(flux, 1, axis=axis)
         interior[z] = total
         products = (start * start, start * v, v * v)
-        return tuple(s + fold(p) for s, p in zip(sums, products, strict=True))
-
-    sums = lax.fori_loop(0, NZ, plane_step, (jnp.zeros((8, 128), F32),) * 3)
+        return below, tuple(s + fold(p) for s, p in zip(sums, products, strict=True))
+
+    carry = jnp.zeros((NX, NY), F32), (jnp.zeros((8, 128), F32),) * 3
+    _, sums = lax.fori_loop(0, NZ, plane_step, carry)
     for slot in range(3):
         partial[slot] = sums[slot]
 
@@ -337,56 +349,36 @@
     sums_out[...] = jnp.broadcast_to(row, sums_out.shape)
 
 
-def least_squares(hess, beta):
-    count = len(hess)
-    rows = count + 1
-    nothing = jnp.zeros_like(beta)
-    columns = [[h[i] if i < len(h) else nothing for i in range(rows)] for h in hess]
-    basis_q = []
-    upper_r = [[None] * count for _ in range(count)]
-    for column in range(count):
-        vector = columns[column]
-        for row in range(column):
-            products = [q * c for q, c in zip(basis_q[row], columns[column], strict=True)]
-            upper_r[row][column] = sum(products[1:], products[0])
-        for row in range(column):
-            scale = upper_r[row][column]
-            vector = [v - scale * q for v, q in zip(vector, basis_q[row], strict=True)]
-        squares = [v * v for v in vector]
-        upper_r[column][column] = jnp.sqrt(sum(squares[1:], squares[0]))
-        basis_q.append([v / upper_r[column][column] for v in vector])
-    target = [beta * basis_q[row][0] for row in range(count)]
-    solved = [None] * count
-    for row in range(count - 1, -1, -1):
-        value = target[row]
-        for column in range(row + 1, count):
-            value = value - upper_r[row][column] * solved[column]
-        solved[row] = value / upper_r[row][row]
-    return solved
-
-
 def combine_kernel(rhs, first, second, sums, update_out, residual_out, update, residual, left):
-    total = jnp.sum(sums[...], axis=0, keepdims=True)
-    g00, g01, g11, g02, g12, g22 = (total[:, i : i + 1] for i in range(6))
-    square = g00 + EPS
-    beta = jnp.sqrt(square)
-    h00 = g01 / square
-    rest = (g11 - 2.0 * h00 * g01 + h00 * h00 * g00) / square
-    rest = jnp.maximum(rest, 0.0)
-    h10 = jnp.sqrt(rest + EPS)
-    h01 = (g02 - h00 * g01) / (square * h10)
-    scale = square * h10 * h10
-    h11 = (g12 - h00 * (g02 + g11 - h00 * g01)) / scale
-    norm_w = (g22 - 2.0 * h00 * g12 + h00 * h00 * g11) / scale
-    v00 = g00 / square
-    v01 = (g01 - h00 * g00) / (square * h10)
-    v11 = rest / (h10 * h10)
-    last = norm_w - 2.0 * (h01 * h01 + h11 * h11)
-    last = last + h01 * h01 * v00 + 2.0 * h01 * h11 * v01 + h11 * h11 * v11
-    h21 = jnp.sqrt(jnp.maximum(last, 0.0) + EPS)
-    y0, y1 = least_squares([[h00, h10], [h01, h11, h21]], beta)
-    step = y1 / (beta * h10)
-    base = y0 / beta - h00 * step
+    total = jnp.sum(sums[...].reshape(-1, 8, 8), axis=0)
+    total = jnp.sum(total, axis=0, keepdims=True)
+    g00, g01, g11, g02, g12, g22 = (
+        jnp.broadcast_to(total[:, i : i + 1], (8, 128)) for i in range(6)
+    )
+    over = 1.0 / (g00 + EPS)
+    h00 = g01 * over
+    rest = jnp.maximum((g11 - h00 * (2.0 * g01 - h00 * g00)) * over, 0.0)
+    p = rest + EPS
+    over_p = 1.0 / p
+    over_n0 = 1.0 / (h00 * h00 + p)
+    h01p = (g02 - h00 * g01) * over
+    h11p = (g12 - h00 * (g02 + g11 - h00 * g01)) * over
+    h11 = h11p * over_p
+    h01_h01 = h01p * h01p * over_p
+    norm_w = (g22 - h00 * (2.0 * g12 - h00 * g11)) * over * over_p
+    v01p = (g01 - h00 * g00) * over
+    last = norm_w + h01_h01 * (g00 * over - 2.0) + h11 * h11 * (rest * over_p - 2.0)
+    last = last + 2.0 * (h01p * over_p) * h11 * v01p
+    h21_h21 = jnp.maximum(last, 0.0) + EPS
+    c = (h00 * h01p + h11p) * over_n0
+    v0 = h01p - c * h00
+    v1 = h11 - c
+    n1 = v0 * v0 * over_p + v1 * v1 + h21_h21
+    step = v0 * over_p / n1
+    base = h00 * over_n0 - (c + h00) * step
+    base, step = (
+        jnp.concatenate([jnp.concatenate([x] * 2, axis=1)] * TILES, axis=0) for x in (base, step)
+    )
 
     def plane_step(z, carry):
         a, b, c = rhs[z], first[z], second[z]
@@ -432,32 +424,31 @@
         scratch_shapes=list(scratch),
         compiler_params=PARAMS,
         cost_estimate=cost(flops),
-        name=kernel.__name__,
-    )
-
-
-def body(head, soil, boundary, rhs, soil_alpha, soil_n, soil_ks):
+    )
+
+
+def iterations(head, soil, boundary, rhs, soil_alpha, soil_n, soil_ks):
     whole = shape(*BLOCK)
     counts = jax.ShapeDtypeStruct(BLOCK, jnp.int32)
     sides = (shape(3, NX, NY), shape(3, 8, NY), shape(3, 8, NY), shape(3, 8, 128))
-    sources = (head, soil, boundary, rhs, soil_alpha, soil_n, soil_ks)
+    sources = (head, soil, rhs, soil_alpha, soil_n, soil_ks, boundary)
     sources = [pltpu.with_memory_space_constraint(x, pltpu.HBM) for x in sources]
-    head, soil, boundary, rhs, tables, z, xa, xb, y = call(
+    head, soil, rhs, tables, z, xa, xb, y = call(
         pack_kernel,
-        [HBM] * 7,
-        (whole, counts, counts, whole, shape(4, 8, 128)) + sides,
+        [HBM] * 6,
+        (whole, counts, whole, shape(4, 8, 128)) + sides,
         1000000,
-        scratch=[pltpu.SMEM((SOILS,), F32)] * 3 + [pltpu.SemaphoreType.DMA((7,))],
-    )(*sources)
+        scratch=[pltpu.SMEM((SOILS,), F32)] * 3 + [pltpu.SemaphoreType.DMA((6,))],
+    )(*sources[:6])
     far = exchange(z, xa, xb, y)
     own = (shape(2, NX, NY), shape(2, 2, 8, NY), shape(2, 8, 128))
-    coeffs, interior, own_z, own_x, own_y = call(
+    coeffs, interior, own_z, own_x, own_y, boundary = call(
         terms_kernel,
-        [VMEM] * 7,
-        (shape(7, *BLOCK), whole) + own,
+        [VMEM] * 7 + [HBM],
+        (shape(7, *BLOCK), whole) + own + (counts,),
         40000000,
-        scratch=[pltpu.VMEM(BLOCK, F32)] * 2,
-    )(head, soil, rhs, xa, xb, y, tables)
+        scratch=[pltpu.VMEM((NZ + 1, NX, NY), F32)] * 2 + [pltpu.SemaphoreType.DMA],
+    )(head, soil, rhs, xa, xb, y, tables, sources[6])
     sides = (shape(NX, NY), shape(8, NY), shape(8, NY), shape(8, 128))
     first, z1, xa1, xb1, y1, face_z, face_x, face_y = call(
         first_kernel, [VMEM] * 17, (whole,) + sides + own, 8000000
@@ -484,4 +475,4 @@
     split = Mesh(mesh.devices.reshape(4, 4, 4, 2, mesh.shape["gz"]), AXES)
     in_specs = (P("gz", GX, GY),) * 4 + (P(), P(), P())
     out_specs = (P("gz", GX, GY), P("gz", GX, GY))
-    return jax.shard_map(body, mesh=split, in_specs=in_specs, out_specs=out_specs, check_vma=False)
+    return jax.shard_map(iterations, mesh=split, in_specs=in_specs, out_specs=out_specs, check_vma=False)

time: 52.8 us -> 51.6 us (0.977)
  Pallas kernels: 9.94 us -> 8.37 us
  blocking collectives: 22.7 us -> 23.6 us
    pallas_call x6, Pallas kernels: 9.94 us -> 8.37 us  [the longest x1 2.76 us: iterations(): call(terms_kernel, [VMEM] * 7 + [HBM], (shape(7, *BLOCK), whole) + own +...]
    all_to_all x1, blocking collectives: 22.7 us -> 23.6 us  [iterations(): sums = lax.all_to_all(sums, AXES, 0, 0)]
  transfers between devices with their start and end apart: 10 -> 10, of which waited for: 2 -> 1; matrix products, arithmetic and copies ran while one was open for 0% -> 0% of each run, Pallas kernels for 9% -> 8%
where the time goes in v2:
time: 51.6 us; the launch traced here: 51.5 us
  blocking collectives  23.6 us (46%)
  starting transfers between devices  18.4 us (36%)
  Pallas kernels  8.37 us (16%)
  between operations  0.74 us (1%)
    all_to_all x1, blocking collectives, iterations(): sums = lax.all_to_all(sums, AXES, 0, 0)  23.6 us
    ppermute x10, starting transfers between devices, swap(): return lax.ppermute(x, axis, pairs + [(b, a) for a, b in pairs])  18.4 us
    pallas_call x1, Pallas kernels, iterations(): call(terms_kernel, [VMEM] * 7 + [HBM], (shape(7, *BLOCK), whole) + own +...  2.76 us
    pallas_call x1, Pallas kernels, iterations(): call(pack_kernel, [HBM] * 6, (whole, counts, whole, shape(4, 8, 128)) + s...  1.72 us
    pallas_call x1, Pallas kernels, iterations(): call(inner_kernel, [VMEM] * 3, (whole, shape(3, 8, 128)), 8000000)  1.36 us
    pallas_call x1, Pallas kernels, iterations(): call(combine_kernel, [VMEM] * 4, (whole, whole), 1000000, (HBM, HBM), [pl...  1.24 us
  transfers between devices with their start and end apart: 10, of which 1 were waited for; matrix products, arithmetic and copies ran while one was open for 0% of the time, Pallas kernels for 8%

profile of v2, /device:TPU:1, one launch (start us, length us, event | category | flops | bytes accessed | tf_op | source)
XLA Modules:
  0.0 51.5 jit_solution(7653054653238929360)
XLA Ops:
  0.6 1.7 %shard_map.86 = (f32[8,64,256]{2,1,0:T(8,128)S(1)}, s32[8,64,256]{2,1,0:T(8,128)S(1)}, f32[8,64,256]{2,1,0:T(8,128)S(1)}, f32[4,8,128]{2,1,0:T(8,128)S(1)}, f32[...) custom-call(f32[8,64,256]{2,1,0:T(8,128)} %head.1, ...), custom_call_target="tpu_custom_call" | custom-call | flops 1000000 | bytes 4194304 | tf_op jit(solution)/shard_map/pallas_call | solution.py:436
  2.4 2.5 %collective-permute-start = (f32[3,64,256]{2,1,0:T(8,128)S(1)}, f32[3,64,256]{2,1,0:T(8,128)S(1)}, u32[]{:S(2)}, u32[]{:S(2)}) collective-permute-start(f32[3,64,256]{2,1,0:T(8,128)S(1)} %get-tuple-element.37.z_own), channel_id=1, source_target_pairs={{0,1},{1,0},{2,3},{3,2},{4,5},{5,4},{6,7},{7,6},{8,9},{9,8},{10,11... | collective-permute-start | bytes 589832 | tf_op jit(solution)/shard_map/ppermute | solution.py:404
  4.9 1.2 %collective-permute-start.1 = (f32[3,8,256]{2,1,0:T(8,128)S(1)}, f32[3,8,256]{2,1,0:T(8,128)S(1)}, u32[]{:S(2)}, u32[]{:S(2)}) collective-permute-start(f32[3,8,256]{2,1,0:T(8,128)S(1)} %get-tuple-element.31.xa.xa_own), channel_id=1, source_target_pairs={{0,16},{32,48},{64,80},{96,112},{128,144},{160,176},{192,208},{224... | collective-permute-start | bytes 73736 | tf_op jit(solution)/shard_map/ppermute | solution.py:404
  6.1 4.3 %collective-permute-start.2 = (f32[3,8,256]{2,1,0:T(8,128)S(1)}, f32[3,8,256]{2,1,0:T(8,128)S(1)}, u32[]{:S(2)}, u32[]{:S(2)}) collective-permute-start(f32[3,8,256]{2,1,0:T(8,128)S(1)} %get-tuple-element.32.xb.xb_own), channel_id=1, source_target_pairs={{16,32},{48,64},{80,96},{112,128},{144,160},{176,192},{208,224},{2... | collective-permute-start | bytes 73736 | tf_op jit(solution)/shard_map/ppermute | solution.py:404
  10.4 4.4 %collective-permute-start.4 = (f32[3,8,128]{2,1,0:T(8,128)S(1)}, f32[3,8,128]{2,1,0:T(8,128)S(1)}, u32[]{:S(2)}, u32[]{:S(2)}) collective-permute-start(f32[3,8,128]{2,1,0:T(8,128)S(1)} %get-tuple-element.33.y.y_own), channel_id=1, source_target_pairs={{2,4},{6,8},{10,12},{14,0},{4,2},{8,6},{12,10},{0,14},{3,5},{7,9},... | collective-permute-start | bytes 36872 | tf_op jit(solution)/shard_map/ppermute | solution.py:404
  14.8 1.1 %collective-permute-start.3 = (f32[3,8,128]{2,1,0:T(8,128)S(1)}, f32[3,8,128]{2,1,0:T(8,128)S(1)}, u32[]{:S(2)}, u32[]{:S(2)}) collective-permute-start(f32[3,8,128]{2,1,0:T(8,128)S(1)} %get-tuple-element.33.y.y_own), channel_id=1, source_target_pairs={{0,2},{4,6},{8,10},{12,14},{2,0},{6,4},{10,8},{14,12},{1,3},{5,7},... | collective-permute-start | bytes 36872 | tf_op jit(solution)/shard_map/ppermute | solution.py:404
  15.9 2.8 %shard_map.87 = (f32[7,8,64,256]{3,2,1,0:T(8,128)S(1)}, f32[8,64,256]{2,1,0:T(8,128)S(1)}, f32[2,64,256]{2,1,0:T(8,128)S(1)}, f32[2,2,8,256]{3,2,1,0:T(8,128)S(1...) custom-call(f32[8,64,256]{2,1,0:T(8,128)S(1)} %get-tuple-element.29.head, ...), custom_call_target="tpu_custom_call" | custom-call | flops 40000000 | bytes 4194304 | tf_op jit(solution)/shard_map/pallas_call | solution.py:445
  18.7 0.0 collective-permute-done.4.yb_far
  18.7 0.0 collective-permute-done.3.ya_far
  18.7 0.0 collective-permute-done.1.xa_far
  18.7 0.0 collective-permute-done.2.xb_far
  18.7 0.0 collective-permute-done.z_far
  18.7 0.8 %shard_map.88 = (f32[8,64,256]{2,1,0:T(8,128)S(1)}, f32[64,256]{1,0:T(8,128)S(1)}, f32[8,256]{1,0:T(8,128)S(1)}, f32[8,256]{1,0:T(8,128)S(1)}, f32[8,128]{1,0:T(...) custom-call(f32[8,64,256]{2,1,0:T(8,128)S(1)} %get-tuple-element.29.head, ...), custom_call_target="tpu_custom_call" | custom-call | flops 8000000 | bytes 4194304 | tf_op jit(solution)/shard_map/pallas_call | solution.py:453
  19.5 0.8 %collective-permute-start.5 = (f32[64,256]{1,0:T(8,128)S(1)}, f32[64,256]{1,0:T(8,128)S(1)}, u32[]{:S(2)}, u32[]{:S(2)}) collective-permute-start(f32[64,256]{1,0:T(8,128)S(1)} %get-tuple-element.45.z_own), channel_id=1, source_target_pairs={{0,1},{1,0},{2,3},{3,2},{4,5},{5,4},{6,7},{7,6},{8,9},{9,8},{10,11... | collective-permute-start | bytes 196616 | tf_op jit(solution)/shard_map/ppermute | solution.py:404
  20.3 0.0 collective-permute-start.6
  20.3 0.9 %collective-permute-start.7 = (f32[8,256]{1,0:T(8,128)S(1)}, f32[8,256]{1,0:T(8,128)S(1)}, u32[]{:S(2)}, u32[]{:S(2)}) collective-permute-start(f32[8,256]{1,0:T(8,128)S(1)} %get-tuple-element.47.xb_own), channel_id=1, source_target_pairs={{16,32},{48,64},{80,96},{112,128},{144,160},{176,192},{208,224},{2... | collective-permute-start | bytes 24584 | tf_op jit(solution)/shard_map/ppermute | solution.py:404
  21.3 3.1 %collective-permute-start.9 = (f32[8,128]{1,0:T(8,128)S(1)}, f32[8,128]{1,0:T(8,128)S(1)}, u32[]{:S(2)}, u32[]{:S(2)}) collective-permute-start(f32[8,128]{1,0:T(8,128)S(1)} %get-tuple-element.48.y_own), channel_id=1, source_target_pairs={{2,4},{6,8},{10,12},{14,0},{4,2},{8,6},{12,10},{0,14},{3,5},{7,9},... | collective-permute-start | bytes 12296 | tf_op jit(solution)/shard_map/ppermute | solution.py:404
  24.4 0.0 collective-permute-start.8
  24.4 1.4 %shard_map.89 = (f32[8,64,256]{2,1,0:T(8,128)S(1)}, f32[3,8,128]{2,1,0:T(8,128)S(1)}) custom-call(f32[7,8,64,256]{3,2,1,0:T(8,128)S(1)} %get-tuple-element.42.coeffs, f32[8,64,256]{2,1,0:T(8,128)S(1)} %get-tuple-element.41.v_ref.first, f32[8,64,256]{2,1,0:T(8,128)S(1)} %get-tuple-element.28.rhs), custom_call_target="tpu_custom_call" | custom-call | flops 8000000 | bytes 4194304 | tf_op jit(solution)/shard_map/pallas_call | solution.py:457
  25.8 0.0 collective-permute-done.9.yb_far
  25.8 0.0 collective-permute-done.8.ya_far
  25.8 0.0 collective-permute-done.6.xa_far
  25.8 0.4 collective-permute-done.7.xb_far
  26.2 0.0 collective-permute-done.5.z_far
  26.2 0.5 shard_map.90
  26.7 23.6 %all_to_all.11 = f32[256,1,8]{2,1,0:T(1,128)S(1)} all-to-all(f32[256,1,8]{2,1,0:T(1,128)S(1)} %bitcast.5), channel_id=1, replica_groups=mesh['gx_0'=4,'gx_1'=4,'gy_0'=4,'gy_1'=2,'gz'=2] {'gx_0','gx_1','gy_0','..., dimensions={0} | all-to-all | bytes 16384 | tf_op jit(solution)/shard_map/all_to_all | solution.py:463
  50.2 1.2 %shard_map.91 = (f32[8,64,256]{2,1,0:T(8,128)}, f32[8,64,256]{2,1,0:T(8,128)}) custom-call(f32[8,64,256]{2,1,0:T(8,128)S(1)} %get-tuple-element.28.rhs, f32[8,64,256]{2,1,0:T(8,128)S(1)} %get-tuple-element.41.v_ref.first, f32[8,64,256]{2,1,0:T(8,128)S(1)} %get-tuple-element.52.second, f32[256,8]{1,0:T(8,128)S(1)} %bitcast.4), custom_call_target="tpu_custom_call" | custom-call | flops 1000000 | bytes 4194304 | tf_op jit(solution)/shard_map/pallas_call | solution.py:464
Async XLA Ops:
  2.4 16.4 %collective-permute-start = (f32[3,64,256]{2,1,0:T(8,128)S(1)}, f32[3,64,256]{2,1,0:T(8,128)S(1)}, u32[]{:S(2)}, u32[]{:S(2)}) collective-permute-start(f32[3,64,256]{2,1,0:T(8,128)S(1)} %get-tuple-element.37.z_own), channel_id=1, source_target_pairs={{0,1},{1,0},{2,3},{3,2},{4,5},{5,4},{6,7},{7,6},{8,9},{9,8},{10,11... | collective-permute-start | bytes 589832 | tf_op jit(solution)/shard_map/ppermute | solution.py:404
  4.9 13.8 %collective-permute-start.1 = (f32[3,8,256]{2,1,0:T(8,128)S(1)}, f32[3,8,256]{2,1,0:T(8,128)S(1)}, u32[]{:S(2)}, u32[]{:S(2)}) collective-permute-start(f32[3,8,256]{2,1,0:T(8,128)S(1)} %get-tuple-element.31.xa.xa_own), channel_id=1, source_target_pairs={{0,16},{32,48},{64,80},{96,112},{128,144},{160,176},{192,208},{224... | collective-permute-start | bytes 73736 | tf_op jit(solution)/shard_map/ppermute | solution.py:404
  6.1 12.6 %collective-permute-start.2 = (f32[3,8,256]{2,1,0:T(8,128)S(1)}, f32[3,8,256]{2,1,0:T(8,128)S(1)}, u32[]{:S(2)}, u32[]{:S(2)}) collective-permute-start(f32[3,8,256]{2,1,0:T(8,128)S(1)} %get-tuple-element.32.xb.xb_own), channel_id=1, source_target_pairs={{16,32},{48,64},{80,96},{112,128},{144,160},{176,192},{208,224},{2... | collective-permute-start | bytes 73736 | tf_op jit(solution)/shard_map/ppermute | solution.py:404
  10.4 8.3 %collective-permute-start.4 = (f32[3,8,128]{2,1,0:T(8,128)S(1)}, f32[3,8,128]{2,1,0:T(8,128)S(1)}, u32[]{:S(2)}, u32[]{:S(2)}) collective-permute-start(f32[3,8,128]{2,1,0:T(8,128)S(1)} %get-tuple-element.33.y.y_own), channel_id=1, source_target_pairs={{2,4},{6,8},{10,12},{14,0},{4,2},{8,6},{12,10},{0,14},{3,5},{7,9},... | collective-permute-start | bytes 36872 | tf_op jit(solution)/shard_map/ppermute | solution.py:404
  14.8 3.9 %collective-permute-start.3 = (f32[3,8,128]{2,1,0:T(8,128)S(1)}, f32[3,8,128]{2,1,0:T(8,128)S(1)}, u32[]{:S(2)}, u32[]{:S(2)}) collective-permute-start(f32[3,8,128]{2,1,0:T(8,128)S(1)} %get-tuple-element.33.y.y_own), channel_id=1, source_target_pairs={{0,2},{4,6},{8,10},{12,14},{2,0},{6,4},{10,8},{14,12},{1,3},{5,7},... | collective-permute-start | bytes 36872 | tf_op jit(solution)/shard_map/ppermute | solution.py:404
  19.5 6.7 %collective-permute-start.5 = (f32[64,256]{1,0:T(8,128)S(1)}, f32[64,256]{1,0:T(8,128)S(1)}, u32[]{:S(2)}, u32[]{:S(2)}) collective-permute-start(f32[64,256]{1,0:T(8,128)S(1)} %get-tuple-element.45.z_own), channel_id=1, source_target_pairs={{0,1},{1,0},{2,3},{3,2},{4,5},{5,4},{6,7},{7,6},{8,9},{9,8},{10,11... | collective-permute-start | bytes 196616 | tf_op jit(solution)/shard_map/ppermute | solution.py:404
  20.3 5.4 %collective-permute-start.6 = (f32[8,256]{1,0:T(8,128)S(1)}, f32[8,256]{1,0:T(8,128)S(1)}, u32[]{:S(2)}, u32[]{:S(2)}) collective-permute-start(f32[8,256]{1,0:T(8,128)S(1)} %get-tuple-element.46.xa_own), channel_id=1, source_target_pairs={{0,16},{32,48},{64,80},{96,112},{128,144},{160,176},{192,208},{224... | collective-permute-start | bytes 24584 | tf_op jit(solution)/shard_map/ppermute | solution.py:404
  20.3 5.8 %collective-permute-start.7 = (f32[8,256]{1,0:T(8,128)S(1)}, f32[8,256]{1,0:T(8,128)S(1)}, u32[]{:S(2)}, u32[]{:S(2)}) collective-permute-start(f32[8,256]{1,0:T(8,128)S(1)} %get-tuple-element.47.xb_own), channel_id=1, source_target_pairs={{16,32},{48,64},{80,96},{112,128},{144,160},{176,192},{208,224},{2... | collective-permute-start | bytes 24584 | tf_op jit(solution)/shard_map/ppermute | solution.py:404
  21.3 4.5 %collective-permute-start.9 = (f32[8,128]{1,0:T(8,128)S(1)}, f32[8,128]{1,0:T(8,128)S(1)}, u32[]{:S(2)}, u32[]{:S(2)}) collective-permute-start(f32[8,128]{1,0:T(8,128)S(1)} %get-tuple-element.48.y_own), channel_id=1, source_target_pairs={{2,4},{6,8},{10,12},{14,0},{4,2},{8,6},{12,10},{0,14},{3,5},{7,9},... | collective-permute-start | bytes 12296 | tf_op jit(solution)/shard_map/ppermute | solution.py:404
  24.4 1.4 %collective-permute-start.8 = (f32[8,128]{1,0:T(8,128)S(1)}, f32[8,128]{1,0:T(8,128)S(1)}, u32[]{:S(2)}, u32[]{:S(2)}) collective-permute-start(f32[8,128]{1,0:T(8,128)S(1)} %get-tuple-element.48.y_own), channel_id=1, source_target_pairs={{0,2},{4,6},{8,10},{12,14},{2,0},{6,4},{10,8},{14,12},{1,3},{5,7},... | collective-permute-start | bytes 12296 | tf_op jit(solution)/shard_map/ppermute | solution.py:404

commit v3 on v2

--- a/solution.py
+++ b/solution.py
@@ -87,7 +87,24 @@
     return lax.broadcasted_iota(jnp.int32, dims, len(dims) - 2)
 
 
-def gather_columns(plane, z, first_at, last_at, packed):
+def gather_columns(plane, z):
+    lane = lane_index((8, 128))
+    packed = jnp.zeros((8, 128), F32)
+    for tile in range(TILES):
+        rows = slice(8 * tile, 8 * tile + 8)
+        at = TILES * z + tile
+        first = pltpu.roll(plane[rows, 0:128], at, axis=1) if at else plane[rows, 0:128]
+        last = pltpu.roll(plane[rows, NY - 128 : NY], (at + 65) % 128, axis=1)
+        packed = jnp.where(lane == at, first, packed)
+        packed = jnp.where(lane == at + 64, last, packed)
+    return packed
+
+
+def column_lanes(odd_y):
+    return jnp.where(odd_y, 0, 64), jnp.where(odd_y, 64, 0)
+
+
+def add_columns(plane, z, first_at, last_at, packed):
     lane = lane_index((8, 128))
     for tile in range(TILES):
         rows = slice(8 * tile, 8 * tile + 8)
@@ -98,6 +115,16 @@
     return packed
 
 
+def tree(parts):
+    while len(parts) > 1:
+        parts = [a + b for a, b in zip(parts[::2], parts[1::2], strict=True)]
+    return parts[0]
+
+
+def by_phase(packed, odd_y):
+    return jnp.where(odd_y, packed, pltpu.roll(packed, 64, axis=1))
+
+
 def gather_rows(plane, odd_x):
     low, high = plane[0:1, :], plane[NX - 1 : NX, :]
     return jnp.where(odd_x, low, high), jnp.where(odd_x, high, low)
@@ -105,13 +132,13 @@
 
 def spread_sides(z, odd_x, odd_y, row_a, row_b, packed):
     low, high = jnp.where(odd_x, row_a, row_b), jnp.where(odd_x, row_b, row_a)
-    first = jnp.where(odd_y, packed, pltpu.roll(packed, 64, axis=1))
+    first = by_phase(packed, odd_y)
     lane, row = lane_index((8, 128)), row_index((8, NY))
     pieces = []
     for tile in range(TILES):
         at = TILES * z + tile
-        left = jnp.broadcast_to(first[:, at : at + 1], (8, 128))
-        right = jnp.broadcast_to(first[:, at + 64 : at + 65], (8, 128))
+        left = pltpu.roll(first, (128 - at) % 128, axis=1)
+        right = pltpu.roll(first, 63 - at, axis=1)
         left, right = jnp.where(lane == 0, left, 0.0), jnp.where(lane == 127, right, 0.0)
         piece = jnp.concatenate([left, right], axis=1)
         if tile == 0:
@@ -124,10 +151,6 @@
 
 def odd_sides():
     return (lax.axis_index("gx_1") % 2) == 1, lax.axis_index("gy_1") == 1
-
-
-def column_lanes(odd_y):
-    return jnp.where(odd_y, 0, 64), jnp.where(odd_y, 64, 0)
 
 
 def pack_kernel(
@@ -167,7 +190,7 @@
         packed = jnp.zeros((8, 128), F32)
         for z in range(NZ):
             plane = ref[z].astype(F32)
-            packed = gather_columns(plane, z, first_at, last_at, packed)
+            packed = add_columns(plane, z, first_at, last_at, packed)
             row_a, row_b = gather_rows(plane, odd_x)
             xa_out[slot, z : z + 1, :] = row_a
             xb_out[slot, z : z + 1, :] = row_b
@@ -274,8 +297,7 @@
     image[...] = interior[...]
     image[edge] = image[edge] + sum_z
 
-    first_at, last_at = column_lanes(odd_y)
-    packed = jnp.zeros((8, 128), F32)
+    columns = []
     for z in range(NZ):
         total = image[z] + spread_sides(
             z, odd_x, odd_y, sums_x[0][z : z + 1, :], sums_x[1][z : z + 1, :], sum_y
@@ -285,8 +307,8 @@
         row_a, row_b = gather_rows(plane, odd_x)
         xa_out[z : z + 1, :] = row_a
         xb_out[z : z + 1, :] = row_b
-        packed = gather_columns(plane, z, first_at, last_at, packed)
-    y_out[...] = packed
+        columns.append(gather_columns(plane, z))
+    y_out[...] = by_phase(tree(columns), odd_y)
     z_out[...] = image[edge]
 
 
@@ -313,7 +335,7 @@
         return below, tuple(s + fold(p) for s, p in zip(sums, products, strict=True))
 
     carry = jnp.zeros((NX, NY), F32), (jnp.zeros((8, 128), F32),) * 3
-    _, sums = lax.fori_loop(0, NZ, plane_step, carry)
+    _, sums = lax.fori_loop(0, NZ, plane_step, carry, unroll=True)
     for slot in range(3):
         partial[slot] = sums[slot]
 

time: 51.6 us -> 51.3 us (level)
  Pallas kernels: 8.37 us -> 7.51 us
  waiting for transfers between devices: 0.39 us -> 1.02 us
    ppermute x10, waiting for transfers between devices: 0.39 us -> 1.02 us  [swap(): return lax.ppermute(x, axis, pairs + [(b, a) for a, b in pairs])]
    pallas_call x1, Pallas kernels: 1.36 us -> 0.75 us  [iterations(): call(inner_kernel, [VMEM] * 3, (whole, shape(3, 8, 128)), 8000000)]
  transfers between devices with their start and end apart: 10 -> 10, of which waited for: 1 -> 2; matrix products, arithmetic and copies ran while one was open for 0% -> 0% of each run, Pallas kernels for 8% -> 7%
where the time goes in v3:
time: 51.3 us; the launch traced here: 51.2 us
  blocking collectives  23.6 us (46%)
  starting transfers between devices  18.3 us (36%)
  Pallas kernels  7.51 us (15%)
  waiting for transfers between devices  1.02 us (2%)
  between operations  0.71 us (1%)
    all_to_all x1, blocking collectives, iterations(): sums = lax.all_to_all(sums, AXES, 0, 0)  23.6 us
    ppermute x10, starting transfers between devices, swap(): return lax.ppermute(x, axis, pairs + [(b, a) for a, b in pairs])  18.3 us
    pallas_call x1, Pallas kernels, iterations(): call(terms_kernel, [VMEM] * 7 + [HBM], (shape(7, *BLOCK), whole) + own +...  2.76 us
    pallas_call x1, Pallas kernels, iterations(): call(pack_kernel, [HBM] * 6, (whole, counts, whole, shape(4, 8, 128)) + s...  1.72 us
    pallas_call x1, Pallas kernels, iterations(): call(combine_kernel, [VMEM] * 4, (whole, whole), 1000000, (HBM, HBM), [pl...  1.24 us
  transfers between devices with their start and end apart: 10, of which 2 were waited for; matrix products, arithmetic and copies ran while one was open for 0% of the time, Pallas kernels for 7%

profile of v3, /device:TPU:1, one launch (start us, length us, event | category | flops | bytes accessed | tf_op | source)
XLA Modules:
  0.0 51.2 jit_solution(13599794256136372790)
XLA Ops:
  0.6 1.7 %shard_map.86 = (f32[8,64,256]{2,1,0:T(8,128)S(1)}, s32[8,64,256]{2,1,0:T(8,128)S(1)}, f32[8,64,256]{2,1,0:T(8,128)S(1)}, f32[4,8,128]{2,1,0:T(8,128)S(1)}, f32[...) custom-call(f32[8,64,256]{2,1,0:T(8,128)} %head.1, ...), custom_call_target="tpu_custom_call" | custom-call | flops 1000000 | bytes 4194304 | tf_op jit(solution)/shard_map/pallas_call | solution.py:458
  2.4 2.5 %collective-permute-start = (f32[3,64,256]{2,1,0:T(8,128)S(1)}, f32[3,64,256]{2,1,0:T(8,128)S(1)}, u32[]{:S(2)}, u32[]{:S(2)}) collective-permute-start(f32[3,64,256]{2,1,0:T(8,128)S(1)} %get-tuple-element.37.z_own), channel_id=1, source_target_pairs={{0,1},{1,0},{2,3},{3,2},{4,5},{5,4},{6,7},{7,6},{8,9},{9,8},{10,11... | collective-permute-start | bytes 589832 | tf_op jit(solution)/shard_map/ppermute | solution.py:426
  4.9 1.2 %collective-permute-start.1 = (f32[3,8,256]{2,1,0:T(8,128)S(1)}, f32[3,8,256]{2,1,0:T(8,128)S(1)}, u32[]{:S(2)}, u32[]{:S(2)}) collective-permute-start(f32[3,8,256]{2,1,0:T(8,128)S(1)} %get-tuple-element.31.xa.xa_own), channel_id=1, source_target_pairs={{0,16},{32,48},{64,80},{96,112},{128,144},{160,176},{192,208},{224... | collective-permute-start | bytes 73736 | tf_op jit(solution)/shard_map/ppermute | solution.py:426
  6.1 4.3 %collective-permute-start.2 = (f32[3,8,256]{2,1,0:T(8,128)S(1)}, f32[3,8,256]{2,1,0:T(8,128)S(1)}, u32[]{:S(2)}, u32[]{:S(2)}) collective-permute-start(f32[3,8,256]{2,1,0:T(8,128)S(1)} %get-tuple-element.32.xb.xb_own), channel_id=1, source_target_pairs={{16,32},{48,64},{80,96},{112,128},{144,160},{176,192},{208,224},{2... | collective-permute-start | bytes 73736 | tf_op jit(solution)/shard_map/ppermute | solution.py:426
  10.4 4.4 %collective-permute-start.4 = (f32[3,8,128]{2,1,0:T(8,128)S(1)}, f32[3,8,128]{2,1,0:T(8,128)S(1)}, u32[]{:S(2)}, u32[]{:S(2)}) collective-permute-start(f32[3,8,128]{2,1,0:T(8,128)S(1)} %get-tuple-element.33.y.y_own), channel_id=1, source_target_pairs={{2,4},{6,8},{10,12},{14,0},{4,2},{8,6},{12,10},{0,14},{3,5},{7,9},... | collective-permute-start | bytes 36872 | tf_op jit(solution)/shard_map/ppermute | solution.py:426
  14.8 1.1 %collective-permute-start.3 = (f32[3,8,128]{2,1,0:T(8,128)S(1)}, f32[3,8,128]{2,1,0:T(8,128)S(1)}, u32[]{:S(2)}, u32[]{:S(2)}) collective-permute-start(f32[3,8,128]{2,1,0:T(8,128)S(1)} %get-tuple-element.33.y.y_own), channel_id=1, source_target_pairs={{0,2},{4,6},{8,10},{12,14},{2,0},{6,4},{10,8},{14,12},{1,3},{5,7},... | collective-permute-start | bytes 36872 | tf_op jit(solution)/shard_map/ppermute | solution.py:426
  15.9 2.8 %shard_map.87 = (f32[7,8,64,256]{3,2,1,0:T(8,128)S(1)}, f32[8,64,256]{2,1,0:T(8,128)S(1)}, f32[2,64,256]{2,1,0:T(8,128)S(1)}, f32[2,2,8,256]{3,2,1,0:T(8,128)S(1...) custom-call(f32[8,64,256]{2,1,0:T(8,128)S(1)} %get-tuple-element.29.head, ...), custom_call_target="tpu_custom_call" | custom-call | flops 40000000 | bytes 4194304 | tf_op jit(solution)/shard_map/pallas_call | solution.py:467
  18.7 0.0 collective-permute-done.4.yb_far
  18.7 0.0 collective-permute-done.3.ya_far
  18.7 0.0 collective-permute-done.1.xa_far
  18.7 0.0 collective-permute-done.2.xb_far
  18.7 0.0 collective-permute-done.z_far
  18.7 0.6 %shard_map.88 = (f32[8,64,256]{2,1,0:T(8,128)S(1)}, f32[64,256]{1,0:T(8,128)S(1)}, f32[8,256]{1,0:T(8,128)S(1)}, f32[8,256]{1,0:T(8,128)S(1)}, f32[8,128]{1,0:T(...) custom-call(f32[8,64,256]{2,1,0:T(8,128)S(1)} %get-tuple-element.29.head, ...), custom_call_target="tpu_custom_call" | custom-call | flops 8000000 | bytes 4194304 | tf_op jit(solution)/shard_map/pallas_call | solution.py:475
  19.3 0.8 %collective-permute-start.5 = (f32[64,256]{1,0:T(8,128)S(1)}, f32[64,256]{1,0:T(8,128)S(1)}, u32[]{:S(2)}, u32[]{:S(2)}) collective-permute-start(f32[64,256]{1,0:T(8,128)S(1)} %get-tuple-element.45.z_own), channel_id=1, source_target_pairs={{0,1},{1,0},{2,3},{3,2},{4,5},{5,4},{6,7},{7,6},{8,9},{9,8},{10,11... | collective-permute-start | bytes 196616 | tf_op jit(solution)/shard_map/ppermute | solution.py:426
  20.1 0.0 collective-permute-start.6
  20.1 0.9 %collective-permute-start.7 = (f32[8,256]{1,0:T(8,128)S(1)}, f32[8,256]{1,0:T(8,128)S(1)}, u32[]{:S(2)}, u32[]{:S(2)}) collective-permute-start(f32[8,256]{1,0:T(8,128)S(1)} %get-tuple-element.47.xb_own), channel_id=1, source_target_pairs={{16,32},{48,64},{80,96},{112,128},{144,160},{176,192},{208,224},{2... | collective-permute-start | bytes 24584 | tf_op jit(solution)/shard_map/ppermute | solution.py:426
  21.0 3.1 %collective-permute-start.9 = (f32[8,128]{1,0:T(8,128)S(1)}, f32[8,128]{1,0:T(8,128)S(1)}, u32[]{:S(2)}, u32[]{:S(2)}) collective-permute-start(f32[8,128]{1,0:T(8,128)S(1)} %get-tuple-element.48.y_own), channel_id=1, source_target_pairs={{2,4},{6,8},{10,12},{14,0},{4,2},{8,6},{12,10},{0,14},{3,5},{7,9},... | collective-permute-start | bytes 12296 | tf_op jit(solution)/shard_map/ppermute | solution.py:426
  24.1 0.0 collective-permute-start.8
  24.1 0.8 %shard_map.89 = (f32[8,64,256]{2,1,0:T(8,128)S(1)}, f32[3,8,128]{2,1,0:T(8,128)S(1)}) custom-call(f32[7,8,64,256]{3,2,1,0:T(8,128)S(1)} %get-tuple-element.42.coeffs, f32[8,64,256]{2,1,0:T(8,128)S(1)} %get-tuple-element.41.v_ref.first, f32[8,64,256]{2,1,0:T(8,128)S(1)} %get-tuple-element.28.rhs), custom_call_target="tpu_custom_call" | custom-call | flops 8000000 | bytes 4194304 | tf_op jit(solution)/shard_map/pallas_call | solution.py:479
  24.9 0.5 %collective-permute-done.9.yb_far = f32[8,128]{1,0:T(8,128)S(1)} collective-permute-done((f32[8,128]{1,0:T(8,128)S(1)}, f32[8,128]{1,0:T(8,128)S(1)}, u32[]{:S(2)}, u32[]{:S(2)}) %collective-permute-start.9) | collective-permute-done | bytes 4128 | tf_op jit(solution)/shard_map/ppermute | solution.py:426
  25.4 0.0 collective-permute-done.8.ya_far
  25.4 0.0 collective-permute-done.6.xa_far
  25.4 0.5 collective-permute-done.7.xb_far
  25.9 0.0 collective-permute-done.5.z_far
  25.9 0.4 shard_map.90
  26.3 23.6 %all_to_all.11 = f32[256,1,8]{2,1,0:T(1,128)S(1)} all-to-all(f32[256,1,8]{2,1,0:T(1,128)S(1)} %bitcast.5), channel_id=1, replica_groups=mesh['gx_0'=4,'gx_1'=4,'gy_0'=4,'gy_1'=2,'gz'=2] {'gx_0','gx_1','gy_0','..., dimensions={0} | all-to-all | bytes 16384 | tf_op jit(solution)/shard_map/all_to_all | solution.py:485
  49.9 1.2 %shard_map.91 = (f32[8,64,256]{2,1,0:T(8,128)}, f32[8,64,256]{2,1,0:T(8,128)}) custom-call(f32[8,64,256]{2,1,0:T(8,128)S(1)} %get-tuple-element.28.rhs, f32[8,64,256]{2,1,0:T(8,128)S(1)} %get-tuple-element.41.v_ref.first, f32[8,64,256]{2,1,0:T(8,128)S(1)} %get-tuple-element.52.second, f32[256,8]{1,0:T(8,128)S(1)} %bitcast.4), custom_call_target="tpu_custom_call" | custom-call | flops 1000000 | bytes 4194304 | tf_op jit(solution)/shard_map/pallas_call | solution.py:486
Async XLA Ops:
  2.4 16.4 %collective-permute-start = (f32[3,64,256]{2,1,0:T(8,128)S(1)}, f32[3,64,256]{2,1,0:T(8,128)S(1)}, u32[]{:S(2)}, u32[]{:S(2)}) collective-permute-start(f32[3,64,256]{2,1,0:T(8,128)S(1)} %get-tuple-element.37.z_own), channel_id=1, source_target_pairs={{0,1},{1,0},{2,3},{3,2},{4,5},{5,4},{6,7},{7,6},{8,9},{9,8},{10,11... | collective-permute-start | bytes 589832 | tf_op jit(solution)/shard_map/ppermute | solution.py:426
  4.9 13.8 %collective-permute-start.1 = (f32[3,8,256]{2,1,0:T(8,128)S(1)}, f32[3,8,256]{2,1,0:T(8,128)S(1)}, u32[]{:S(2)}, u32[]{:S(2)}) collective-permute-start(f32[3,8,256]{2,1,0:T(8,128)S(1)} %get-tuple-element.31.xa.xa_own), channel_id=1, source_target_pairs={{0,16},{32,48},{64,80},{96,112},{128,144},{160,176},{192,208},{224... | collective-permute-start | bytes 73736 | tf_op jit(solution)/shard_map/ppermute | solution.py:426
  6.1 12.6 %collective-permute-start.2 = (f32[3,8,256]{2,1,0:T(8,128)S(1)}, f32[3,8,256]{2,1,0:T(8,128)S(1)}, u32[]{:S(2)}, u32[]{:S(2)}) collective-permute-start(f32[3,8,256]{2,1,0:T(8,128)S(1)} %get-tuple-element.32.xb.xb_own), channel_id=1, source_target_pairs={{16,32},{48,64},{80,96},{112,128},{144,160},{176,192},{208,224},{2... | collective-permute-start | bytes 73736 | tf_op jit(solution)/shard_map/ppermute | solution.py:426
  10.4 8.3 %collective-permute-start.4 = (f32[3,8,128]{2,1,0:T(8,128)S(1)}, f32[3,8,128]{2,1,0:T(8,128)S(1)}, u32[]{:S(2)}, u32[]{:S(2)}) collective-permute-start(f32[3,8,128]{2,1,0:T(8,128)S(1)} %get-tuple-element.33.y.y_own), channel_id=1, source_target_pairs={{2,4},{6,8},{10,12},{14,0},{4,2},{8,6},{12,10},{0,14},{3,5},{7,9},... | collective-permute-start | bytes 36872 | tf_op jit(solution)/shard_map/ppermute | solution.py:426
  14.8 3.9 %collective-permute-start.3 = (f32[3,8,128]{2,1,0:T(8,128)S(1)}, f32[3,8,128]{2,1,0:T(8,128)S(1)}, u32[]{:S(2)}, u32[]{:S(2)}) collective-permute-start(f32[3,8,128]{2,1,0:T(8,128)S(1)} %get-tuple-element.33.y.y_own), channel_id=1, source_target_pairs={{0,2},{4,6},{8,10},{12,14},{2,0},{6,4},{10,8},{14,12},{1,3},{5,7},... | collective-permute-start | bytes 36872 | tf_op jit(solution)/shard_map/ppermute | solution.py:426
  19.3 6.6 %collective-permute-start.5 = (f32[64,256]{1,0:T(8,128)S(1)}, f32[64,256]{1,0:T(8,128)S(1)}, u32[]{:S(2)}, u32[]{:S(2)}) collective-permute-start(f32[64,256]{1,0:T(8,128)S(1)} %get-tuple-element.45.z_own), channel_id=1, source_target_pairs={{0,1},{1,0},{2,3},{3,2},{4,5},{5,4},{6,7},{7,6},{8,9},{9,8},{10,11... | collective-permute-start | bytes 196616 | tf_op jit(solution)/shard_map/ppermute | solution.py:426
  20.1 5.3 %collective-permute-start.6 = (f32[8,256]{1,0:T(8,128)S(1)}, f32[8,256]{1,0:T(8,128)S(1)}, u32[]{:S(2)}, u32[]{:S(2)}) collective-permute-start(f32[8,256]{1,0:T(8,128)S(1)} %get-tuple-element.46.xa_own), channel_id=1, source_target_pairs={{0,16},{32,48},{64,80},{96,112},{128,144},{160,176},{192,208},{224... | collective-permute-start | bytes 24584 | tf_op jit(solution)/shard_map/ppermute | solution.py:426
  20.1 5.8 %collective-permute-start.7 = (f32[8,256]{1,0:T(8,128)S(1)}, f32[8,256]{1,0:T(8,128)S(1)}, u32[]{:S(2)}, u32[]{:S(2)}) collective-permute-start(f32[8,256]{1,0:T(8,128)S(1)} %get-tuple-element.47.xb_own), channel_id=1, source_target_pairs={{16,32},{48,64},{80,96},{112,128},{144,160},{176,192},{208,224},{2... | collective-permute-start | bytes 24584 | tf_op jit(solution)/shard_map/ppermute | solution.py:426
  21.0 4.4 %collective-permute-start.9 = (f32[8,128]{1,0:T(8,128)S(1)}, f32[8,128]{1,0:T(8,128)S(1)}, u32[]{:S(2)}, u32[]{:S(2)}) collective-permute-start(f32[8,128]{1,0:T(8,128)S(1)} %get-tuple-element.48.y_own), channel_id=1, source_target_pairs={{2,4},{6,8},{10,12},{14,0},{4,2},{8,6},{12,10},{0,14},{3,5},{7,9},... | collective-permute-start | bytes 12296 | tf_op jit(solution)/shard_map/ppermute | solution.py:426
  24.1 1.3 %collective-permute-start.8 = (f32[8,128]{1,0:T(8,128)S(1)}, f32[8,128]{1,0:T(8,128)S(1)}, u32[]{:S(2)}, u32[]{:S(2)}) collective-permute-start(f32[8,128]{1,0:T(8,128)S(1)} %get-tuple-element.48.y_own), channel_id=1, source_target_pairs={{0,2},{4,6},{8,10},{12,14},{2,0},{6,4},{10,8},{14,12},{1,3},{5,7},... | collective-permute-start | bytes 12296 | tf_op jit(solution)/shard_map/ppermute | solution.py:426

commit v4 on v3

--- a/solution.py
+++ b/solution.py
@@ -16,6 +16,7 @@
 PORE = 0.4
 STEP = 0.25
 F32 = jnp.float32
+UNROLL = 8
 LOG2E = 1.4426950408889634
 NZ, NX, NY = 8, 64, 256
 BLOCK = (NZ, NX, NY)
@@ -253,7 +254,7 @@
         image[z] = total
         return below
 
-    lax.fori_loop(0, NZ, faces_step, nothing)
+    lax.fori_loop(0, NZ, faces_step, nothing, unroll=UNROLL)
     copy.wait()
 
 
@@ -294,12 +295,12 @@
         sums_x.append(total)
     near, away, sum_z = face(z_own, (own_z[0], own_z[1]), z_far, None, tilt)
     face_z[0], face_z[1] = near, away
-    image[...] = interior[...]
-    image[edge] = image[edge] + sum_z
+    at_edge = {0: jnp.where(gz == 0, 0.0, sum_z), NZ - 1: jnp.where(gz == 0, sum_z, 0.0)}
 
     columns = []
     for z in range(NZ):
-        total = image[z] + spread_sides(
+        total = interior[z] + at_edge[z] if z in at_edge else interior[z]
+        total = total + spread_sides(
             z, odd_x, odd_y, sums_x[0][z : z + 1, :], sums_x[1][z : z + 1, :], sum_y
         )
         plane = jnp.where(boundary[z] == 1, rhs[z], total)
@@ -346,17 +347,18 @@
     image, sums_out,
 ):
     odd_x, odd_y = odd_sides()
-    edge = jnp.where(lax.axis_index("gz") == 0, NZ - 1, 0)
+    gz = lax.axis_index("gz")
     sum_y = face_y[0] * y_own[...] + face_y[1] * pick_y(ya_far[...], yb_far[...])
     sum_xa = face_x[0, 0] * xa_own[...] + face_x[0, 1] * xa_far[...]
     sum_xb = face_x[1, 0] * xb_own[...] + face_x[1, 1] * xb_far[...]
-    image[...] = interior[...]
-    image[edge] = image[edge] + face_z[0] * z_own[...] + face_z[1] * z_far[...]
+    sum_z = face_z[0] * z_own[...] + face_z[1] * z_far[...]
+    at_edge = {0: jnp.where(gz == 0, 0.0, sum_z), NZ - 1: jnp.where(gz == 0, sum_z, 0.0)}
 
     sums = None
     for z in range(NZ):
         v = v_ref[z]
-        total = image[z] + spread_sides(
+        total = interior[z] + at_edge[z] if z in at_edge else interior[z]
+        total = total + spread_sides(
             z, odd_x, odd_y, sum_xa[z : z + 1, :], sum_xb[z : z + 1, :], sum_y
         )
         plane = jnp.where(boundary[z] == 1, v, total)

time: 51.3 us -> 51.3 us (level)
  transfers between devices with their start and end apart: 10 -> 10, of which waited for: 2 -> 2; matrix products, arithmetic and copies ran while one was open for 0% -> 0% of each run, Pallas kernels for 7% -> 6%
where the time goes in v4:
time: 51.3 us; the launch traced here: 51.2 us
  blocking collectives  24 us (47%)
  starting transfers between devices  18.3 us (36%)
  Pallas kernels  7.12 us (14%)
  waiting for transfers between devices  1.02 us (2%)
  between operations  0.71 us (1%)
    all_to_all x1, blocking collectives, iterations(): sums = lax.all_to_all(sums, AXES, 0, 0)  24 us
    ppermute x10, starting transfers between devices, swap(): return lax.ppermute(x, axis, pairs + [(b, a) for a, b in pairs])  18.3 us
    pallas_call x1, Pallas kernels, iterations(): call(terms_kernel, [VMEM] * 7 + [HBM], (shape(7, *BLOCK), whole) + own +...  2.35 us
    pallas_call x1, Pallas kernels, iterations(): call(pack_kernel, [HBM] * 6, (whole, counts, whole, shape(4, 8, 128)) + s...  1.72 us
    pallas_call x1, Pallas kernels, iterations(): call(combine_kernel, [VMEM] * 4, (whole, whole), 1000000, (HBM, HBM), [pl...  1.24 us
  transfers between devices with their start and end apart: 10, of which 2 were waited for; matrix products, arithmetic and copies ran while one was open for 0% of the time, Pallas kernels for 6%

profile of v4, /device:TPU:1, one launch (start us, length us, event | category | flops | bytes accessed | tf_op | source)
XLA Modules:
  0.0 51.2 jit_solution(3958427299948894555)
XLA Ops:
  0.6 1.7 %shard_map.86 = (f32[8,64,256]{2,1,0:T(8,128)S(1)}, s32[8,64,256]{2,1,0:T(8,128)S(1)}, f32[8,64,256]{2,1,0:T(8,128)S(1)}, f32[4,8,128]{2,1,0:T(8,128)S(1)}, f32[...) custom-call(f32[8,64,256]{2,1,0:T(8,128)} %head.1, ...), custom_call_target="tpu_custom_call" | custom-call | flops 1000000 | bytes 4194304 | tf_op jit(solution)/shard_map/pallas_call | solution.py:460
  2.4 2.5 %collective-permute-start = (f32[3,64,256]{2,1,0:T(8,128)S(1)}, f32[3,64,256]{2,1,0:T(8,128)S(1)}, u32[]{:S(2)}, u32[]{:S(2)}) collective-permute-start(f32[3,64,256]{2,1,0:T(8,128)S(1)} %get-tuple-element.37.z_own), channel_id=1, source_target_pairs={{0,1},{1,0},{2,3},{3,2},{4,5},{5,4},{6,7},{7,6},{8,9},{9,8},{10,11... | collective-permute-start | bytes 589832 | tf_op jit(solution)/shard_map/ppermute | solution.py:428
  4.9 1.2 %collective-permute-start.1 = (f32[3,8,256]{2,1,0:T(8,128)S(1)}, f32[3,8,256]{2,1,0:T(8,128)S(1)}, u32[]{:S(2)}, u32[]{:S(2)}) collective-permute-start(f32[3,8,256]{2,1,0:T(8,128)S(1)} %get-tuple-element.31.xa.xa_own), channel_id=1, source_target_pairs={{0,16},{32,48},{64,80},{96,112},{128,144},{160,176},{192,208},{224... | collective-permute-start | bytes 73736 | tf_op jit(solution)/shard_map/ppermute | solution.py:428
  6.1 4.3 %collective-permute-start.2 = (f32[3,8,256]{2,1,0:T(8,128)S(1)}, f32[3,8,256]{2,1,0:T(8,128)S(1)}, u32[]{:S(2)}, u32[]{:S(2)}) collective-permute-start(f32[3,8,256]{2,1,0:T(8,128)S(1)} %get-tuple-element.32.xb.xb_own), channel_id=1, source_target_pairs={{16,32},{48,64},{80,96},{112,128},{144,160},{176,192},{208,224},{2... | collective-permute-start | bytes 73736 | tf_op jit(solution)/shard_map/ppermute | solution.py:428
  10.4 4.4 %collective-permute-start.4 = (f32[3,8,128]{2,1,0:T(8,128)S(1)}, f32[3,8,128]{2,1,0:T(8,128)S(1)}, u32[]{:S(2)}, u32[]{:S(2)}) collective-permute-start(f32[3,8,128]{2,1,0:T(8,128)S(1)} %get-tuple-element.33.y.y_own), channel_id=1, source_target_pairs={{2,4},{6,8},{10,12},{14,0},{4,2},{8,6},{12,10},{0,14},{3,5},{7,9},... | collective-permute-start | bytes 36872 | tf_op jit(solution)/shard_map/ppermute | solution.py:428
  14.8 1.1 %collective-permute-start.3 = (f32[3,8,128]{2,1,0:T(8,128)S(1)}, f32[3,8,128]{2,1,0:T(8,128)S(1)}, u32[]{:S(2)}, u32[]{:S(2)}) collective-permute-start(f32[3,8,128]{2,1,0:T(8,128)S(1)} %get-tuple-element.33.y.y_own), channel_id=1, source_target_pairs={{0,2},{4,6},{8,10},{12,14},{2,0},{6,4},{10,8},{14,12},{1,3},{5,7},... | collective-permute-start | bytes 36872 | tf_op jit(solution)/shard_map/ppermute | solution.py:428
  15.9 2.4 %shard_map.87 = (f32[7,8,64,256]{3,2,1,0:T(8,128)S(1)}, f32[8,64,256]{2,1,0:T(8,128)S(1)}, f32[2,64,256]{2,1,0:T(8,128)S(1)}, f32[2,2,8,256]{3,2,1,0:T(8,128)S(1...) custom-call(f32[8,64,256]{2,1,0:T(8,128)S(1)} %get-tuple-element.29.head, ...), custom_call_target="tpu_custom_call" | custom-call | flops 40000000 | bytes 4194304 | tf_op jit(solution)/shard_map/pallas_call | solution.py:469
  18.3 0.0 collective-permute-done.4.yb_far
  18.3 0.0 collective-permute-done.3.ya_far
  18.3 0.0 collective-permute-done.1.xa_far
  18.3 0.0 collective-permute-done.2.xb_far
  18.3 0.0 collective-permute-done.z_far
  18.3 0.6 %shard_map.88 = (f32[8,64,256]{2,1,0:T(8,128)S(1)}, f32[64,256]{1,0:T(8,128)S(1)}, f32[8,256]{1,0:T(8,128)S(1)}, f32[8,256]{1,0:T(8,128)S(1)}, f32[8,128]{1,0:T(...) custom-call(f32[8,64,256]{2,1,0:T(8,128)S(1)} %get-tuple-element.29.head, ...), custom_call_target="tpu_custom_call" | custom-call | flops 8000000 | bytes 4194304 | tf_op jit(solution)/shard_map/pallas_call | solution.py:477
  18.9 0.7 %collective-permute-start.5 = (f32[64,256]{1,0:T(8,128)S(1)}, f32[64,256]{1,0:T(8,128)S(1)}, u32[]{:S(2)}, u32[]{:S(2)}) collective-permute-start(f32[64,256]{1,0:T(8,128)S(1)} %get-tuple-element.45.z_own), channel_id=1, source_target_pairs={{0,1},{1,0},{2,3},{3,2},{4,5},{5,4},{6,7},{7,6},{8,9},{9,8},{10,11... | collective-permute-start | bytes 196616 | tf_op jit(solution)/shard_map/ppermute | solution.py:428
  19.7 0.0 collective-permute-start.6
  19.7 0.9 %collective-permute-start.7 = (f32[8,256]{1,0:T(8,128)S(1)}, f32[8,256]{1,0:T(8,128)S(1)}, u32[]{:S(2)}, u32[]{:S(2)}) collective-permute-start(f32[8,256]{1,0:T(8,128)S(1)} %get-tuple-element.47.xb_own), channel_id=1, source_target_pairs={{16,32},{48,64},{80,96},{112,128},{144,160},{176,192},{208,224},{2... | collective-permute-start | bytes 24584 | tf_op jit(solution)/shard_map/ppermute | solution.py:428
  20.6 3.1 %collective-permute-start.9 = (f32[8,128]{1,0:T(8,128)S(1)}, f32[8,128]{1,0:T(8,128)S(1)}, u32[]{:S(2)}, u32[]{:S(2)}) collective-permute-start(f32[8,128]{1,0:T(8,128)S(1)} %get-tuple-element.48.y_own), channel_id=1, source_target_pairs={{2,4},{6,8},{10,12},{14,0},{4,2},{8,6},{12,10},{0,14},{3,5},{7,9},... | collective-permute-start | bytes 12296 | tf_op jit(solution)/shard_map/ppermute | solution.py:428
  23.7 0.0 collective-permute-start.8
  23.7 0.8 %shard_map.89 = (f32[8,64,256]{2,1,0:T(8,128)S(1)}, f32[3,8,128]{2,1,0:T(8,128)S(1)}) custom-call(f32[7,8,64,256]{3,2,1,0:T(8,128)S(1)} %get-tuple-element.42.coeffs, f32[8,64,256]{2,1,0:T(8,128)S(1)} %get-tuple-element.41.v_ref.first, f32[8,64,256]{2,1,0:T(8,128)S(1)} %get-tuple-element.28.rhs), custom_call_target="tpu_custom_call" | custom-call | flops 8000000 | bytes 4194304 | tf_op jit(solution)/shard_map/pallas_call | solution.py:481
  24.5 0.5 %collective-permute-done.9.yb_far = f32[8,128]{1,0:T(8,128)S(1)} collective-permute-done((f32[8,128]{1,0:T(8,128)S(1)}, f32[8,128]{1,0:T(8,128)S(1)}, u32[]{:S(2)}, u32[]{:S(2)}) %collective-permute-start.9) | collective-permute-done | bytes 4128 | tf_op jit(solution)/shard_map/ppermute | solution.py:428
  25.0 0.0 collective-permute-done.8.ya_far
  25.0 0.0 collective-permute-done.6.xa_far
  25.0 0.5 collective-permute-done.7.xb_far
  25.5 0.0 collective-permute-done.5.z_far
  25.5 0.5 shard_map.90
  25.9 24.0 %all_to_all.11 = f32[256,1,8]{2,1,0:T(1,128)S(1)} all-to-all(f32[256,1,8]{2,1,0:T(1,128)S(1)} %bitcast.5), channel_id=1, replica_groups=mesh['gx_0'=4,'gx_1'=4,'gy_0'=4,'gy_1'=2,'gz'=2] {'gx_0','gx_1','gy_0','..., dimensions={0} | all-to-all | bytes 16384 | tf_op jit(solution)/shard_map/all_to_all | solution.py:487
  49.9 1.2 %shard_map.91 = (f32[8,64,256]{2,1,0:T(8,128)}, f32[8,64,256]{2,1,0:T(8,128)}) custom-call(f32[8,64,256]{2,1,0:T(8,128)S(1)} %get-tuple-element.28.rhs, f32[8,64,256]{2,1,0:T(8,128)S(1)} %get-tuple-element.41.v_ref.first, f32[8,64,256]{2,1,0:T(8,128)S(1)} %get-tuple-element.52.second, f32[256,8]{1,0:T(8,128)S(1)} %bitcast.4), custom_call_target="tpu_custom_call" | custom-call | flops 1000000 | bytes 4194304 | tf_op jit(solution)/shard_map/pallas_call | solution.py:488
Async XLA Ops:
  2.4 15.9 %collective-permute-start = (f32[3,64,256]{2,1,0:T(8,128)S(1)}, f32[3,64,256]{2,1,0:T(8,128)S(1)}, u32[]{:S(2)}, u32[]{:S(2)}) collective-permute-start(f32[3,64,256]{2,1,0:T(8,128)S(1)} %get-tuple-element.37.z_own), channel_id=1, source_target_pairs={{0,1},{1,0},{2,3},{3,2},{4,5},{5,4},{6,7},{7,6},{8,9},{9,8},{10,11... | collective-permute-start | bytes 589832 | tf_op jit(solution)/shard_map/ppermute | solution.py:428
  4.9 13.4 %collective-permute-start.1 = (f32[3,8,256]{2,1,0:T(8,128)S(1)}, f32[3,8,256]{2,1,0:T(8,128)S(1)}, u32[]{:S(2)}, u32[]{:S(2)}) collective-permute-start(f32[3,8,256]{2,1,0:T(8,128)S(1)} %get-tuple-element.31.xa.xa_own), channel_id=1, source_target_pairs={{0,16},{32,48},{64,80},{96,112},{128,144},{160,176},{192,208},{224... | collective-permute-start | bytes 73736 | tf_op jit(solution)/shard_map/ppermute | solution.py:428
  6.1 12.2 %collective-permute-start.2 = (f32[3,8,256]{2,1,0:T(8,128)S(1)}, f32[3,8,256]{2,1,0:T(8,128)S(1)}, u32[]{:S(2)}, u32[]{:S(2)}) collective-permute-start(f32[3,8,256]{2,1,0:T(8,128)S(1)} %get-tuple-element.32.xb.xb_own), channel_id=1, source_target_pairs={{16,32},{48,64},{80,96},{112,128},{144,160},{176,192},{208,224},{2... | collective-permute-start | bytes 73736 | tf_op jit(solution)/shard_map/ppermute | solution.py:428
  10.4 7.9 %collective-permute-start.4 = (f32[3,8,128]{2,1,0:T(8,128)S(1)}, f32[3,8,128]{2,1,0:T(8,128)S(1)}, u32[]{:S(2)}, u32[]{:S(2)}) collective-permute-start(f32[3,8,128]{2,1,0:T(8,128)S(1)} %get-tuple-element.33.y.y_own), channel_id=1, source_target_pairs={{2,4},{6,8},{10,12},{14,0},{4,2},{8,6},{12,10},{0,14},{3,5},{7,9},... | collective-permute-start | bytes 36872 | tf_op jit(solution)/shard_map/ppermute | solution.py:428
  14.8 3.5 %collective-permute-start.3 = (f32[3,8,128]{2,1,0:T(8,128)S(1)}, f32[3,8,128]{2,1,0:T(8,128)S(1)}, u32[]{:S(2)}, u32[]{:S(2)}) collective-permute-start(f32[3,8,128]{2,1,0:T(8,128)S(1)} %get-tuple-element.33.y.y_own), channel_id=1, source_target_pairs={{0,2},{4,6},{8,10},{12,14},{2,0},{6,4},{10,8},{14,12},{1,3},{5,7},... | collective-permute-start | bytes 36872 | tf_op jit(solution)/shard_map/ppermute | solution.py:428
  18.9 6.6 %collective-permute-start.5 = (f32[64,256]{1,0:T(8,128)S(1)}, f32[64,256]{1,0:T(8,128)S(1)}, u32[]{:S(2)}, u32[]{:S(2)}) collective-permute-start(f32[64,256]{1,0:T(8,128)S(1)} %get-tuple-element.45.z_own), channel_id=1, source_target_pairs={{0,1},{1,0},{2,3},{3,2},{4,5},{5,4},{6,7},{7,6},{8,9},{9,8},{10,11... | collective-permute-start | bytes 196616 | tf_op jit(solution)/shard_map/ppermute | solution.py:428
  19.7 5.3 %collective-permute-start.6 = (f32[8,256]{1,0:T(8,128)S(1)}, f32[8,256]{1,0:T(8,128)S(1)}, u32[]{:S(2)}, u32[]{:S(2)}) collective-permute-start(f32[8,256]{1,0:T(8,128)S(1)} %get-tuple-element.46.xa_own), channel_id=1, source_target_pairs={{0,16},{32,48},{64,80},{96,112},{128,144},{160,176},{192,208},{224... | collective-permute-start | bytes 24584 | tf_op jit(solution)/shard_map/ppermute | solution.py:428
  19.7 5.8 %collective-permute-start.7 = (f32[8,256]{1,0:T(8,128)S(1)}, f32[8,256]{1,0:T(8,128)S(1)}, u32[]{:S(2)}, u32[]{:S(2)}) collective-permute-start(f32[8,256]{1,0:T(8,128)S(1)} %get-tuple-element.47.xb_own), channel_id=1, source_target_pairs={{16,32},{48,64},{80,96},{112,128},{144,160},{176,192},{208,224},{2... | collective-permute-start | bytes 24584 | tf_op jit(solution)/shard_map/ppermute | solution.py:428
  20.6 4.4 %collective-permute-start.9 = (f32[8,128]{1,0:T(8,128)S(1)}, f32[8,128]{1,0:T(8,128)S(1)}, u32[]{:S(2)}, u32[]{:S(2)}) collective-permute-start(f32[8,128]{1,0:T(8,128)S(1)} %get-tuple-element.48.y_own), channel_id=1, source_target_pairs={{2,4},{6,8},{10,12},{14,0},{4,2},{8,6},{12,10},{0,14},{3,5},{7,9},... | collective-permute-start | bytes 12296 | tf_op jit(solution)/shard_map/ppermute | solution.py:428
  23.7 1.3 %collective-permute-start.8 = (f32[8,128]{1,0:T(8,128)S(1)}, f32[8,128]{1,0:T(8,128)S(1)}, u32[]{:S(2)}, u32[]{:S(2)}) collective-permute-start(f32[8,128]{1,0:T(8,128)S(1)} %get-tuple-element.48.y_own), channel_id=1, source_target_pairs={{0,2},{4,6},{8,10},{12,14},{2,0},{6,4},{10,8},{14,12},{1,3},{5,7},... | collective-permute-start | bytes 12296 | tf_op jit(solution)/shard_map/ppermute | solution.py:428
